TPU v7x, 256 devices: a whole 4x4x8 slice. The times are simulated.
256 devices in a mesh: sph: 32 (over x, z), ang: 8 (over y, core).
Axes of the slice: x: 4, y: 4, z: 8, core: 2. Of those that a mesh axis runs over, the one named last changes fastest.
Arguments:
- coefficients: bfloat16 [2048, 240, 1024], P(('sph', 'ang')), may hold values from -0.039794922 to 0.039794922
- positions: int32 [2048, 3], P(('sph', 'ang')), may hold values from 0 to 7
- shift_tables: bfloat16 [3, 8, 480, 240], replicated, may hold values from -1.3 to 1.3
- absorb_weight: float32 [2048, 240], P(('sph', 'ang')), may hold values from 0.02 to 0.9, as said below
- incident: float32 [240, 1024], replicated, may hold values from -1.6 to 1.6
- detector: float32 [128, 64], P('sph'), may hold values from 0.002 to 0.18, as said below
Outputs:
- amplitude: float32 [2, 2, 128, 64, 512], P(None, None, 'sph', 'ang')
- cross_sections: float32 [3, 512], P(None, 'ang')
Inputs may be any that keep to these rules, and one draw needn't show every extreme that they name: `absorb_weight`: Positive. `detector`: Positive.
All inputs are finite; a program needn't handle non-finite values.
Results may differ from a plain program's by a relative error of at most 0.0003.
The roundings to bfloat16 on the way count: a program that leaves them out, or rounds other values in their place, can miss the bound.
Values sent between devices are 32-bit elements; how exact they have to be, the bound alone decides.
No kernel may reach another device: no remote copies, remote signals or barrier semaphores. Data moves between devices by JAX's collectives and lax.ppermute only.
A program may use at most 128 MiB of HBM per device.

v0:
```python
import math

import jax
import jax.numpy as jnp
from jax import lax
from jax.sharding import Mesh
from jax.sharding import PartitionSpec as P

ORDER = 10
AZIM = 64
POL_DEV = 4
SPH = ("sph_0", "sph_1")
ANG = ("ang_0", "ang_1")
SPH_ANG = ("sph_0", "sph_1", "ang_0", "ang_1")


def cut_along(shard, dim, size):
    shape = shard.shape
    parts = shard.reshape(*shape[:dim], size, shape[dim] // size, *shape[dim + 1 :])
    return jnp.moveaxis(parts, dim, 0)


def sum_at_owner(shard, axis, dim):
    parts = cut_along(shard, dim, lax.axis_size(axis))
    arrived = lax.all_to_all(parts, axis, split_axis=0, concat_axis=0, tiled=True)
    return arrived.sum(axis=0)


def summed_rows(shard, axes, dim):
    far, near = axes
    parts = cut_along(shard, dim, lax.axis_size(far))
    nearer = sum_at_owner(parts, near, dim + 1)
    arrived = lax.all_to_all(nearer, far, split_axis=0, concat_axis=0, tiled=True)
    return arrived.sum(axis=0)


def rows_for(lines, size):
    spare = -len(lines) % size
    return jnp.pad(lines, [(0, spare)] + [(0, 0)] * (lines.ndim - 1))


def from_everyone(shard, axis):
    size = lax.axis_size(axis)
    return lax.all_to_all(
        jnp.broadcast_to(shard[None], (size, *shard.shape)), axis, 0, 0, tiled=True
    )


def laid_out(parts, dim):
    shape = list(parts.shape[1:])
    shape[dim] *= parts.shape[0]
    return jnp.moveaxis(parts, 0, dim).reshape(shape)


def gathered_by_axis(shard, axes, dim):
    far, near = axes
    leading = from_everyone(shard, far)
    parts = jnp.swapaxes(from_everyone(leading, near), 0, 1)
    return laid_out(parts.reshape(-1, *shard.shape), dim)


def total_of(shard, axes):
    own = summed_rows(rows_for(shard, lax.axis_size(axes[0]) * lax.axis_size(axes[1])), axes, 0)
    whole = gathered_by_axis(own, axes, 0)
    return whole[: len(shard)].reshape(shard.shape)


def packed_total(arrays, axis):
    ravelled, at, done = (jnp.concatenate([a.reshape(-1) for a in arrays]), 0, [])
    so_far = total_of(ravelled, axis)
    for a in arrays:
        done.append(so_far[at : at + a.size].reshape(a.shape))
        at += a.size
    return tuple(done)


def over_copies(shard, axis):
    everything = from_everyone(shard, axis)
    return jnp.sum(everything, axis=0)


def legendre_table(cos_theta, sine_theta, order):
    values = {}
    values[0, 0] = jnp.zeros_like(cos_theta) + 1.0 / math.sqrt(4.0 * math.pi)
    for azim_order in range(order + 1):
        if azim_order > 0:
            factor = -math.sqrt((2.0 * azim_order + 1.0) / (2.0 * azim_order))
            values[azim_order, azim_order] = (
                factor * sine_theta * values[azim_order - 1, azim_order - 1]
            )
        if azim_order + 1 <= order:
            values[azim_order + 1, azim_order] = (
                math.sqrt(2.0 * azim_order + 3.0) * cos_theta * values[azim_order, azim_order]
            )
        for degree in range(azim_order + 2, order + 1):
            upper_coef = math.sqrt(
                (4.0 * degree * degree - 1.0) / (degree * degree - azim_order * azim_order)
            )
            lower_coef = math.sqrt(
                ((degree - 1.0) * (degree - 1.0) - azim_order * azim_order)
                / (4.0 * (degree - 1.0) * (degree - 1.0) - 1.0)
            )
            values[degree, azim_order] = upper_coef * (
                cos_theta * values[degree - 1, azim_order]
                - lower_coef * values[degree - 2, azim_order]
            )
    return values


def angular_basis(polar_index, azim_index, polar_total, azim_total, order):
    theta = (polar_index.astype(jnp.float32) + 0.5) * (math.pi / polar_total)
    azimuth = azim_index.astype(jnp.float32) * (2.0 * math.pi / azim_total)
    cos_theta = jnp.cos(theta)
    sine_theta = jnp.sin(theta)
    legendre_values = legendre_table(cos_theta, sine_theta, order)
    pi_terms = []
    tau_terms = []
    orders_list = []
    phase_real = []
    phase_imag = []
    unit_powers = [(1.0, 0.0), (0.0, -1.0), (-1.0, 0.0), (0.0, 1.0)]
    for degree in range(1, order + 1):
        norm_factor = 1.0 / math.sqrt(degree * (degree + 1.0))
        power_real, power_imag = unit_powers[(degree + 1) % 4]
        for azim_order in range(-degree, degree + 1):
            size_m = abs(azim_order)
            current = legendre_values[degree, size_m]
            if degree - 1 >= size_m:
                previous = legendre_values[degree - 1, size_m]
            else:
                previous = jnp.zeros_like(current)
            link = math.sqrt(
                (2.0 * degree + 1.0)
                * (degree * degree - azim_order * azim_order)
                / (2.0 * degree - 1.0)
            )
            pi_terms.append(azim_order * current / sine_theta)
            tau_terms.append((degree * cos_theta * current - link * previous) / sine_theta)
            orders_list.append(float(azim_order))
            phase_real.append(power_real * norm_factor)
            phase_imag.append(power_imag * norm_factor)
    pi_block = jnp.stack(pi_terms, axis=1)[:, None, :]
    tau_block = jnp.stack(tau_terms, axis=1)[:, None, :]
    orders_row = jnp.array(orders_list, dtype=jnp.float32)
    angle_table = azimuth[:, None] * orders_row[None, :]
    cos_table = jnp.cos(angle_table)
    sin_table = jnp.sin(angle_table)
    scale_real = jnp.array(phase_real, dtype=jnp.float32)[None, :]
    scale_imag = jnp.array(phase_imag, dtype=jnp.float32)[None, :]
    wave_real = (scale_real * cos_table - scale_imag * sin_table)[None, :, :]
    wave_imag = (scale_real * sin_table + scale_imag * cos_table)[None, :, :]
    theta_real = jnp.concatenate([-pi_block * wave_imag, tau_block * wave_real], axis=-1)
    theta_imag = jnp.concatenate([pi_block * wave_real, tau_block * wave_imag], axis=-1)
    phi_real = jnp.concatenate([-tau_block * wave_real, -pi_block * wave_imag], axis=-1)
    phi_imag = jnp.concatenate([-tau_block * wave_imag, pi_block * wave_real], axis=-1)
    real_part = jnp.stack([theta_real, phi_real])
    imag_part = jnp.stack([theta_imag, phi_imag])
    return (real_part, imag_part, sine_theta)


def evaluate_far(real_part, imag_part, anchor):
    half = anchor.shape[1] // 2
    first = jnp.einsum("cikp,pf->cikf", real_part, anchor, precision=lax.Precision.HIGHEST)
    second = jnp.einsum("cikp,pf->cikf", imag_part, anchor, precision=lax.Precision.HIGHEST)
    real_out = first[..., :half] - second[..., half:]
    imag_out = first[..., half:] + second[..., :half]
    return jnp.stack([real_out, imag_out], axis=1)


def rotate_step(matrix, vector):
    product = jnp.einsum("sap,spf->saf", matrix, vector, preferred_element_type=jnp.float32)
    half_rows = matrix.shape[2]
    half_cols = vector.shape[2] // 2
    real_out = product[:, :half_rows, :half_cols] - product[:, half_rows:, half_cols:]
    imag_out = product[:, half_rows:, :half_cols] + product[:, :half_rows, half_cols:]
    return jnp.concatenate([real_out, imag_out], axis=2)


def shards(coefficients, positions, shift_tables, absorb_weight, incident, detector):
    fields = coefficients.shape[2] // 2
    coef_count = coefficients.shape[1]
    along_z = jnp.take(shift_tables[2], positions[:, 2], axis=0)
    along_y = jnp.take(shift_tables[1], positions[:, 1], axis=0)
    along_x = jnp.take(shift_tables[0], positions[:, 0], axis=0)
    first = rotate_step(along_z, coefficients).astype(jnp.bfloat16)
    second = rotate_step(along_y, first).astype(jnp.bfloat16)
    moved = rotate_step(along_x, second)
    partial_value = jnp.sum(moved, axis=0)
    widened = coefficients.astype(jnp.float32)
    squares = widened * widened
    energy = squares[:, :, :fields] + squares[:, :, fields:]
    absorbed = jnp.einsum("sp,spf->f", absorb_weight, energy)
    extinction = jnp.sum(
        incident[:, :fields] * partial_value[:, :fields]
        + incident[:, fields:] * partial_value[:, fields:],
        axis=0,
    )
    local_stats = jnp.stack([extinction, absorbed])
    partial_split = partial_value.reshape(coef_count, 2, fields)
    polar_total = POL_DEV * lax.axis_size(SPH)
    polar_index = lax.axis_index(SPH) * POL_DEV + jnp.arange(POL_DEV)
    groups = lax.axis_size(ANG)
    share = fields // groups
    solid_angle = 2.0 * math.pi * math.pi / (polar_total * AZIM)
    anchor_split, stats = packed_total(
        (partial_split, local_stats), (("sph_0", "sph_1"), ("ang_0", "ang_1"))
    )
    azim_share = AZIM // groups
    azim_start = lax.axis_index(ANG) * azim_share
    azim_index = azim_start + jnp.arange(azim_share)
    real_part, imag_part, sine_theta = angular_basis(
        polar_index, azim_index, polar_total, AZIM, ORDER
    )
    amplitude = evaluate_far(real_part, imag_part, anchor_split.reshape(coef_count, 2 * fields))
    local_detector = lax.dynamic_slice_in_dim(detector, azim_start, azim_share, 1)
    weight = local_detector * sine_theta[:, None] * solid_angle
    power = jnp.einsum("crikf,ik->f", amplitude * amplitude, weight)
    collected = sum_at_owner(power, ANG, 0)
    collected = over_copies(collected, SPH)
    own_stats = lax.dynamic_slice_in_dim(stats, lax.axis_index(ANG) * share, share, 1)
    cross_sections = jnp.concatenate([own_stats, collected[None, :]], axis=0)
    return (amplitude, cross_sections)


def solution(mesh):
    torus = Mesh(mesh.devices.reshape(4, 8, 4, 2), ("sph_0", "sph_1", "ang_0", "ang_1"))
    in_specs = (P(SPH_ANG, None, None), P(SPH_ANG, None), P(), P(SPH_ANG, None), P(), P(SPH, None))
    out_specs = (P(None, None, SPH, ANG, None), P(None, ANG))
    return jax.shard_map(
        shards, mesh=torus, in_specs=in_specs, out_specs=out_specs, check_vma=False
    )
```

profile of v0, /device:TPU:1, one launch (start us, length us, event | category | flops | bytes accessed | tf_op | source)
XLA Modules:
  0.0 190.3 jit_solution(3779762401053682315)
XLA Ops:
  0.6 0.8 compare_and_fusion.2
  1.5 5.5 %slice_bitcast_fusion.2 = (bf16[8,480,240]{2,1,0:T(8,128)(2,1)}, bf16[8,480,240]{2,1,0:T(8,128)(2,1)}, bf16[8,480,240]{2,1,0:T(8,128)(2,1)}) fusion(bf16[3,8,480,240]{3,2,1,0:T(8,128)(2,1)} %param.13), kind=kLoop, calls=%fused_computation.32 | loop fusion | bytes 11059200 | tf_op jit(solution)/shard_map/squeeze | solution.py:184
  7.0 4.2 %convert_multiply_fusion = f32[8,240,1024]{2,1,0:T(8,128)} fusion(bf16[8,240,1024]{2,1,0:T(8,128)(2,1)S(1)} %copy-done.1), kind=kLoop, calls=%fused_computation.4 | loop fusion | flops 3932160 | bytes 11796480 | tf_op jit(solution)/shard_map/mul | solution.py:190
  11.2 2.2 %gather_fusion.2 = bf16[8,480,240]{2,1,0:T(8,128)(2,1)S(1)} fusion(bf16[8,480,240]{2,1,0:T(8,128)(2,1)} %get-tuple-element.26, s32[1024]{0:T(1024)S(1)} %get-tuple-element.51), kind=kCustom, calls=%fused_computation.2.clone | custom fusion | bytes 3686432 | tf_op jit(solution)/shard_map/jit(_take)/gather | solution.py:182
  13.4 9.8 %fusion.14 = f32[8,480,1024]{2,1,0:T(8,128)} fusion(bf16[8,240,1024]{2,1,0:T(8,128)(2,1)} %param.11, bf16[8,480,240]{2,1,0:T(8,128)(2,1)S(1)} %gather_fusion.2, pred[8]{0:T(512)(128)(4,1)S(1)} %get-tuple-element.47), kind=kOutput, calls=%fused_computation.26 | convolution fusion | flops 1888358400 | bytes 21504008 | tf_op jit(solution)/shard_map/sap,spf->saf/dot_general | solution.py:171
  23.2 9.0 %fusion.5 = (bf16[8,240,512]{2,1,0:T(8,128)(2,1)}, bf16[8,240,512]{2,1,0:T(8,128)(2,1)}) fusion(f32[8,480,1024]{2,1,0:T(8,128)} %fusion.14), kind=kLoop, calls=%fused_computation.17 | loop fusion | flops 3932160 | bytes 19660800 | tf_op jit(solution)/shard_map/convert.2
  32.2 2.2 %gather_fusion.1 = bf16[8,480,240]{2,1,0:T(8,128)(2,1)S(1)} fusion(bf16[8,480,240]{2,1,0:T(8,128)(2,1)} %get-tuple-element.27, s32[1024]{0:T(1024)S(1)} %get-tuple-element.52), kind=kCustom, calls=%fused_computation.1.clone | custom fusion | bytes 3686432 | tf_op jit(solution)/shard_map/jit(_take)/gather | solution.py:183
  34.4 9.8 %fusion.6 = f32[8,480,1024]{2,1,0:T(8,128)} fusion(bf16[8,240,512]{2,1,0:T(8,128)(2,1)} %get-tuple-element.24, bf16[8,240,512]{2,1,0:T(8,128)(2,1)} %get-tuple-element.23, bf16[8,480,240]{2,1,0:T(8,128)(2,1)S(1)} %gather_fusion.1, pred[8]{0:T(512)(128)(4,1)S(1)} %get-tuple-element.49), kind=kOutput, calls=%fused_computation.18 | convolution fusion | flops 1896222720 | bytes 21504008 | tf_op jit(solution)/shard_map/sap,spf->saf/dot_general | solution.py:171
  44.3 9.2 %fusion.3 = (bf16[8,240,512]{2,1,0:T(8,128)(2,1)}, bf16[8,240,512]{2,1,0:T(8,128)(2,1)}) fusion(f32[8,480,1024]{2,1,0:T(8,128)} %fusion.6), kind=kLoop, calls=%fused_computation.13 | loop fusion | flops 3932160 | bytes 19660800 | tf_op jit(solution)/shard_map/convert
  53.4 2.2 %gather_fusion = bf16[8,480,240]{2,1,0:T(8,128)(2,1)S(1)} fusion(bf16[8,480,240]{2,1,0:T(8,128)(2,1)} %get-tuple-element.25, s32[1024]{0:T(1024)S(1)} %pad_clamp_fusion.2), kind=kCustom, calls=%fused_computation.clone | custom fusion | bytes 3686432 | tf_op jit(solution)/shard_map/jit(_take)/gather | solution.py:184
  55.7 10.0 %fusion.10 = f32[8,480,1024]{2,1,0:T(8,128)} fusion(bf16[8,240,512]{2,1,0:T(8,128)(2,1)} %get-tuple-element.22, bf16[8,240,512]{2,1,0:T(8,128)(2,1)} %get-tuple-element.21, bf16[8,480,240]{2,1,0:T(8,128)(2,1)S(1)} %gather_fusion, pred[8]{0:T(512)(128)(4,1)S(1)} %get-tuple-element.13), kind=kOutput, calls=%fused_computation.22 | convolution fusion | flops 1896222720 | bytes 21504008 | tf_op jit(solution)/shard_map/sap,spf->saf/dot_general | solution.py:171
  65.7 11.3 %slice_subtract_fusion = (f32[8,240,512]{2,1,0:T(8,128)}, f32[8,240,512]{2,1,0:T(8,128)}) fusion(f32[8,480,1024]{2,1,0:T(8,128)} %fusion.10), kind=kLoop, calls=%fused_computation.9 | loop fusion | flops 1966080 | bytes 23592960 | tf_op jit(solution)/shard_map/sub | solution.py:174
  77.0 4.4 %maximum_reduce_fusion = f32[240,1024]{1,0:T(8,128)S(1)} fusion(f32[8,240,512]{2,1,0:T(8,128)} %get-tuple-element.20, f32[8,240,512]{2,1,0:T(8,128)} %get-tuple-element.19), kind=kLoop, calls=%fused_computation.3 | loop fusion | flops 3686400 | bytes 8847360 | tf_op jit(solution)/shard_map/reduce_sum | solution.py:188
  82.3 0.8 reshape_reshape.9
  83.2 1.6 copy.22
  84.8 6.7 %all-to-all-start = ((f32[8,32,964]{2,1,0:T(8,128)}), f32[8,32,964]{2,1,0:T(8,128)S(1)}, u32[]{:S(2)}, u32[]{:S(2)}) async-start(f32[8,32,964]{2,1,0:T(8,128)} %copy.22), calls=%async_computation | async-start | bytes 2097152 | tf_op jit(solution)/shard_map/all_to_all | solution.py:25
  97.4 9.1 %all-to-all-done = f32[8,32,964]{2,1,0:T(8,128)S(1)} async-done(((f32[8,32,964]{2,1,0:T(8,128)}), f32[8,32,964]{2,1,0:T(8,128)S(1)}, u32[]{:S(2)}, u32[]{:S(2)}) %all-to-all-start) | async-done | bytes 987168 | tf_op jit(solution)/shard_map/all_to_all | solution.py:25
  106.5 0.7 all_to_all.27
  107.3 10.3 %all-to-all-start.1 = ((f32[32,1,964]{2,1,0:T(1,128)}), f32[32,1,964]{2,1,0:T(1,128)S(1)}, u32[]{:S(2)}, u32[]{:S(2)}) async-start(f32[32,1,964]{2,1,0:T(1,128)} %all_to_all.27), calls=%async_computation.1 | async-start | bytes 262144 | tf_op jit(solution)/shard_map/all_to_all | solution.py:33
  117.8 9.0 %all-to-all-done.1 = f32[32,1,964]{2,1,0:T(1,128)S(1)} async-done(((f32[32,1,964]{2,1,0:T(1,128)}), f32[32,1,964]{2,1,0:T(1,128)S(1)}, u32[]{:S(2)}, u32[]{:S(2)}) %all-to-all-start.1) | async-done | bytes 123424 | tf_op jit(solution)/shard_map/all_to_all | solution.py:33
  127.6 3.9 %all-to-all-start.2 = ((f32[32,1,964]{2,1,0:T(1,128)}), f32[32,1,964]{2,1,0:T(1,128)S(1)}, u32[]{:S(2)}, u32[]{:S(2)}) async-start(f32[32,1,964]{2,1,0:T(1,128)} %broadcast_in_dim.19), calls=%async_computation.2 | async-start | bytes 262144 | tf_op jit(solution)/shard_map/all_to_all | solution.py:44
  132.1 8.5 %all-to-all-done.2 = f32[32,1,964]{2,1,0:T(1,128)S(1)} async-done(((f32[32,1,964]{2,1,0:T(1,128)}), f32[32,1,964]{2,1,0:T(1,128)S(1)}, u32[]{:S(2)}, u32[]{:S(2)}) %all-to-all-start.2) | async-done | bytes 123424 | tf_op jit(solution)/shard_map/all_to_all | solution.py:44
  140.6 1.1 broadcast_in_dim.21
  141.7 7.1 %all-to-all-start.3 = ((f32[8,32,964]{2,1,0:T(8,128)}), f32[8,32,964]{2,1,0:T(8,128)S(1)}, u32[]{:S(2)}, u32[]{:S(2)}) async-start(f32[8,32,964]{2,1,0:T(8,128)} %broadcast_in_dim.21), calls=%async_computation.3 | async-start | bytes 2097152 | tf_op jit(solution)/shard_map/all_to_all | solution.py:44
  149.2 14.6 %all-to-all-done.3 = f32[8,32,964]{2,1,0:T(8,128)S(1)} async-done(((f32[8,32,964]{2,1,0:T(8,128)}), f32[8,32,964]{2,1,0:T(8,128)S(1)}, u32[]{:S(2)}, u32[]{:S(2)}) %all-to-all-start.3) | async-done | bytes 987168 | tf_op jit(solution)/shard_map/all_to_all | solution.py:44
  164.4 1.2 slice.120
  167.2 0.8 convolution_bitcast_fusion
  167.9 4.2 %all-to-all-start.4 = ((f32[8,1,64]{2,1,0:T(1,128)}), f32[8,1,64]{2,1,0:T(1,128)S(1)}, u32[]{:S(2)}, u32[]{:S(2)}) async-start(f32[8,1,64]{2,1,0:T(1,128)} %convolution_bitcast_fusion), calls=%async_computation.4 | async-start | bytes 8192 | tf_op jit(solution)/shard_map/all_to_all | solution.py:25
  172.1 1.1 slice.126
  173.3 3.4 %all-to-all-done.4 = f32[8,1,64]{2,1,0:T(1,128)S(1)} async-done(((f32[8,1,64]{2,1,0:T(1,128)}), f32[8,1,64]{2,1,0:T(1,128)S(1)}, u32[]{:S(2)}, u32[]{:S(2)}) %all-to-all-start.4) | async-done | bytes 2080 | tf_op jit(solution)/shard_map/all_to_all | solution.py:25
  177.3 3.7 %all-to-all-start.5 = ((f32[32,1,64]{2,1,0:T(1,128)}), f32[32,1,64]{2,1,0:T(1,128)S(1)}, u32[]{:S(2)}, u32[]{:S(2)}) async-start(f32[32,1,64]{2,1,0:T(1,128)} %broadcast_in_dim.22), calls=%async_computation.5 | async-start | bytes 32768 | tf_op jit(solution)/shard_map/all_to_all | solution.py:44
  181.9 7.9 %all-to-all-done.5 = f32[32,1,64]{2,1,0:T(1,128)S(1)} async-done(((f32[32,1,64]{2,1,0:T(1,128)}), f32[32,1,64]{2,1,0:T(1,128)S(1)}, u32[]{:S(2)}, u32[]{:S(2)}) %all-to-all-start.5) | async-done | bytes 8224 | tf_op jit(solution)/shard_map/all_to_all | solution.py:44
  (148 shorter events, 12.9 us)
Async XLA Ops:
  0.6 81.1 %copy-start = (f32[8,240]{1,0:T(8,128)S(1)}, f32[8,240]{1,0:T(8,128)}, u32[]{:S(2)}) copy-start(f32[8,240]{1,0:T(8,128)} %param.14) | copy-start | bytes 23044
  1.5 5.5 %copy-start.1 = (bf16[8,240,1024]{2,1,0:T(8,128)(2,1)S(1)}, bf16[8,240,1024]{2,1,0:T(8,128)(2,1)}, u32[]{:S(2)}) copy-start(bf16[8,240,1024]{2,1,0:T(8,128)(2,1)} %param.11) | copy-start | bytes 11796484
  55.7 26.1 %slice-start = ((s8[7864320]{0:T(1024)(128)(4,1)}), s8[4194304]{0:T(1024)(128)(4,1)S(1)}, s32[]{:S(2)}) async-start(s8[7864320]{0:T(1024)(128)(4,1)} %bitcast.66), calls=%async_computation.6 | async-start | bytes 8388608
  65.7 16.1 %slice-start.1 = ((s8[7864320]{0:T(1024)(128)(4,1)}), s8[3670016]{0:T(1024)(128)(4,1)S(1)}, s32[]{:S(2)}) async-start(s8[7864320]{0:T(1024)(128)(4,1)} %bitcast.66), calls=%async_computation.7 | async-start | bytes 7340032
  77.0 4.6 %copy-start.2 = (f32[240,1024]{1,0:T(8,128)S(1)}, f32[240,1024]{1,0:T(8,128)}, u32[]{:S(2)}) copy-start(f32[240,1024]{1,0:T(8,128)} %param.15) | copy-start | bytes 2949124
  84.8 21.7 %all-to-all-start = ((f32[8,32,964]{2,1,0:T(8,128)}), f32[8,32,964]{2,1,0:T(8,128)S(1)}, u32[]{:S(2)}, u32[]{:S(2)}) async-start(f32[8,32,964]{2,1,0:T(8,128)} %copy.22), calls=%async_computation | async-start | bytes 2097152 | tf_op jit(solution)/shard_map/all_to_all | solution.py:25
  91.4 57.3 %copy-start.4 = (f32[120]{0:T(128)S(1)}, f32[120]{0:T(128)}, u32[]{:S(2)}) copy-start(f32[120]{0:T(128)} %constant.615.clone) | copy-start | bytes 1444
  91.4 57.3 %copy-start.5 = (f32[120]{0:T(128)S(1)}, f32[120]{0:T(128)}, u32[]{:S(2)}) copy-start(f32[120]{0:T(128)} %constant.616.clone) | copy-start | bytes 1444
  91.4 57.3 %copy-start.6 = (f32[120]{0:T(128)S(1)}, f32[120]{0:T(128)}, u32[]{:S(2)}) copy-start(f32[120]{0:T(128)} %constant.617.clone) | copy-start | bytes 1444
  91.5 57.6 %copy-start.3 = (f32[4,64]{1,0:T(4,128)S(1)}, f32[4,64]{1,0:T(4,128)}, u32[]{:S(2)}) copy-start(f32[4,64]{1,0:T(4,128)} %param.16) | copy-start | bytes 3076
  107.3 19.5 %all-to-all-start.1 = ((f32[32,1,964]{2,1,0:T(1,128)}), f32[32,1,964]{2,1,0:T(1,128)S(1)}, u32[]{:S(2)}, u32[]{:S(2)}) async-start(f32[32,1,964]{2,1,0:T(1,128)} %all_to_all.27), calls=%async_computation.1 | async-start | bytes 262144 | tf_op jit(solution)/shard_map/all_to_all | solution.py:33
  127.6 13.0 %all-to-all-start.2 = ((f32[32,1,964]{2,1,0:T(1,128)}), f32[32,1,964]{2,1,0:T(1,128)S(1)}, u32[]{:S(2)}, u32[]{:S(2)}) async-start(f32[32,1,964]{2,1,0:T(1,128)} %broadcast_in_dim.19), calls=%async_computation.2 | async-start | bytes 262144 | tf_op jit(solution)/shard_map/all_to_all | solution.py:44
  141.7 22.1 %all-to-all-start.3 = ((f32[8,32,964]{2,1,0:T(8,128)}), f32[8,32,964]{2,1,0:T(8,128)S(1)}, u32[]{:S(2)}, u32[]{:S(2)}) async-start(f32[8,32,964]{2,1,0:T(8,128)} %broadcast_in_dim.21), calls=%async_computation.3 | async-start | bytes 2097152 | tf_op jit(solution)/shard_map/all_to_all | solution.py:44
  167.9 8.7 %all-to-all-start.4 = ((f32[8,1,64]{2,1,0:T(1,128)}), f32[8,1,64]{2,1,0:T(1,128)S(1)}, u32[]{:S(2)}, u32[]{:S(2)}) async-start(f32[8,1,64]{2,1,0:T(1,128)} %convolution_bitcast_fusion), calls=%async_computation.4 | async-start | bytes 8192 | tf_op jit(solution)/shard_map/all_to_all | solution.py:25
  177.3 12.4 %all-to-all-start.5 = ((f32[32,1,64]{2,1,0:T(1,128)}), f32[32,1,64]{2,1,0:T(1,128)S(1)}, u32[]{:S(2)}, u32[]{:S(2)}) async-start(f32[32,1,64]{2,1,0:T(1,128)} %broadcast_in_dim.22), calls=%async_computation.5 | async-start | bytes 32768 | tf_op jit(solution)/shard_map/all_to_all | solution.py:44
where the time goes:
time: 191 us; the launch traced here: 190 us
  waiting for transfers between devices  52.4 us (27%)
  other arithmetic  46.2 us (24%)
  starting transfers between devices  35.8 us (19%)
  matrix products  32.3 us (17%)
  local copies, waits for them, and re-layouts  22.3 us (12%)
    all_to_all x3, waiting for transfers between devices, from_everyone(): lax.all_to_all(jnp.broadcast_to(shard[None], (size, *shard.shape)), axis,...  31 us
    dot_general x3, matrix products, rotate_step(): jnp.einsum('sap,spf->saf', matrix, vector, preferred_element_type=jnp.flo...  29.7 us
    another operation x2, other arithmetic  18.2 us
    all_to_all x3, starting transfers between devices, from_everyone(): lax.all_to_all(jnp.broadcast_to(shard[None], (size, *shard.shape)), axis,...  14.7 us
    all_to_all x2, waiting for transfers between devices, sum_at_owner(): lax.all_to_all(parts, axis, split_axis=0, concat_axis=0, tiled=True)  12.5 us
    sub x1, other arithmetic, rotate_step(): product[:, :half_rows, :half_cols] - product[:, half_rows:, half_cols:]  11.3 us
    all_to_all x2, starting transfers between devices, sum_at_owner(): lax.all_to_all(parts, axis, split_axis=0, concat_axis=0, tiled=True)  10.8 us
    all_to_all x1, starting transfers between devices, summed_rows(): lax.all_to_all(nearer, far, split_axis=0, concat_axis=0, tiled=True)  10.3 us
  transfers between devices with their start and end apart: 6, of which 6 were waited for; matrix products, arithmetic and copies ran while one was open for 5% of the time, Pallas kernels for 0%

commit v1 on v0

--- a/solution.py
+++ b/solution.py
@@ -1,8 +1,11 @@
+import functools
 import math
 
 import jax
 import jax.numpy as jnp
 from jax import lax
+from jax.experimental import pallas as pl
+from jax.experimental.pallas import tpu as pltpu
 from jax.sharding import Mesh
 from jax.sharding import PartitionSpec as P
 
@@ -167,29 +170,94 @@
     return jnp.stack([real_out, imag_out], axis=1)
 
 
-def rotate_step(matrix, vector):
-    product = jnp.einsum("sap,spf->saf", matrix, vector, preferred_element_type=jnp.float32)
-    half_rows = matrix.shape[2]
-    half_cols = vector.shape[2] // 2
-    real_out = product[:, :half_rows, :half_cols] - product[:, half_rows:, half_cols:]
-    imag_out = product[:, half_rows:, :half_cols] + product[:, :half_rows, half_cols:]
-    return jnp.concatenate([real_out, imag_out], axis=2)
+COEFS = 240
+FIELDS = 512
+PADDED = 512
+
+
+def move_kernel(unroll, cells_ref, coef_ref, *refs):
+    tables = refs[: 3 * unroll]
+    weight_ref, moved_ref, absorbed_ref, left, right = refs[3 * unroll :]
+    step = pl.program_id(0)
+
+    @pl.when(step == 0)
+    def _():
+        moved_ref[...] = jnp.zeros_like(moved_ref)
+        absorbed_ref[...] = jnp.zeros_like(absorbed_ref)
+        left[...] = jnp.zeros_like(left)
+        right[...] = jnp.zeros_like(right)
+
+    weights = weight_ref[...].T
+    lane = lax.broadcasted_iota(jnp.int32, weights.shape, 1)
+    for s in range(unroll):
+        real, imag = coef_ref[s, :, :FIELDS], coef_ref[s, :, FIELDS:]
+        right[s, :COEFS] = real
+        right[s, 256 : 256 + COEFS] = imag
+        column = jnp.sum(
+            jnp.where(lane == step * unroll + s, weights, 0.0), axis=1, keepdims=True
+        )
+        real, imag = real.astype(jnp.float32), imag.astype(jnp.float32)
+        energy = (real * real + imag * imag) * column
+        absorbed_ref[...] += jnp.sum(energy.reshape(COEFS // 8, 8, FIELDS), axis=0)
+    for stage in range(3):
+        for s in range(unroll):
+            table = tables[stage * unroll + s]
+            left[s, stage, :, :COEFS] = table[0, 0]
+            left[s, stage, :COEFS, 256 : 256 + COEFS] = -table[0, 0, COEFS:]
+            left[s, stage, COEFS:, 256 : 256 + COEFS] = table[0, 0, :COEFS]
+            product = jnp.dot(left[s, stage], right[s], preferred_element_type=jnp.float32)
+            if stage < 2:
+                product = product.astype(jnp.bfloat16)
+                right[s, :COEFS] = product[:COEFS]
+                right[s, 256 : 256 + COEFS] = product[COEFS:]
+            else:
+                moved_ref[...] += product
+
+
+def moved_sum(coefficients, positions, shift_tables, absorb_weight, unroll=2):
+    spheres = coefficients.shape[0]
+
+    def table_of(axis, s):
+        return pl.BlockSpec(
+            (1, 1, 2 * COEFS, COEFS),
+            lambda j, cells: (axis, cells[(j * unroll + s) * 3 + axis], 0, 0),
+        )
+
+    return pl.pallas_call(
+        functools.partial(move_kernel, unroll),
+        grid_spec=pltpu.PrefetchScalarGridSpec(
+            num_scalar_prefetch=1,
+            grid=(spheres // unroll,),
+            in_specs=[pl.BlockSpec((unroll, COEFS, 2 * FIELDS), lambda j, cells: (j, 0, 0))]
+            + [table_of(axis, s) for axis in (2, 1, 0) for s in range(unroll)]
+            + [pl.BlockSpec((spheres, COEFS), lambda j, cells: (0, 0))],
+            out_specs=[
+                pl.BlockSpec((2 * COEFS, FIELDS), lambda j, cells: (0, 0)),
+                pl.BlockSpec((8, FIELDS), lambda j, cells: (0, 0)),
+            ],
+            scratch_shapes=[
+                pltpu.VMEM((unroll, 3, 2 * COEFS, PADDED), jnp.bfloat16),
+                pltpu.VMEM((unroll, PADDED, FIELDS), jnp.bfloat16),
+            ],
+        ),
+        out_shape=[
+            jax.ShapeDtypeStruct((2 * COEFS, FIELDS), jnp.float32),
+            jax.ShapeDtypeStruct((8, FIELDS), jnp.float32),
+        ],
+        compiler_params=pltpu.CompilerParams(dimension_semantics=("arbitrary",)),
+        cost_estimate=pl.CostEstimate(
+            flops=6_000_000_000, bytes_accessed=10_000_000, transcendentals=0
+        ),
+        name="move",
+    )(positions.reshape(-1), coefficients, *([shift_tables] * (3 * unroll)), absorb_weight)
 
 
 def shards(coefficients, positions, shift_tables, absorb_weight, incident, detector):
     fields = coefficients.shape[2] // 2
     coef_count = coefficients.shape[1]
-    along_z = jnp.take(shift_tables[2], positions[:, 2], axis=0)
-    along_y = jnp.take(shift_tables[1], positions[:, 1], axis=0)
-    along_x = jnp.take(shift_tables[0], positions[:, 0], axis=0)
-    first = rotate_step(along_z, coefficients).astype(jnp.bfloat16)
-    second = rotate_step(along_y, first).astype(jnp.bfloat16)
-    moved = rotate_step(along_x, second)
-    partial_value = jnp.sum(moved, axis=0)
-    widened = coefficients.astype(jnp.float32)
-    squares = widened * widened
-    energy = squares[:, :, :fields] + squares[:, :, fields:]
-    absorbed = jnp.einsum("sp,spf->f", absorb_weight, energy)
+    moved, absorbed = moved_sum(coefficients, positions, shift_tables, absorb_weight)
+    absorbed = jnp.sum(absorbed, axis=0)
+    partial_value = jnp.concatenate([moved[:coef_count], moved[coef_count:]], axis=1)
     extinction = jnp.sum(
         incident[:, :fields] * partial_value[:, :fields]
         + incident[:, fields:] * partial_value[:, fields:],

time: 191 us -> 124 us (0.65)
  other arithmetic: 46.2 us -> 8.57 us
  matrix products: 32.3 us -> 2.23 us
  Pallas kernels: 0 us -> 11.3 us
  local copies, waits for them, and re-layouts: 22.3 us -> 11.5 us
    dot_general x4 -> x0, matrix products: 30.1 us -> none  [the longest x3 29.7 us: rotate_step(): jnp.einsum('sap,spf->saf', matrix, vector, preferred_element_type=jnp.flo...]
    another operation x2 -> x0, other arithmetic: 18.2 us -> none
    sub x1 -> x0, other arithmetic: 11.3 us -> none  [rotate_step(): product[:, :half_rows, :half_cols] - product[:, half_rows:, half_cols:]]
    pallas_call x0 -> x1, Pallas kernels: none -> 11.3 us  [moved_sum(): pl.pallas_call(functools.partial(move_kernel, unroll), grid_spec=pltpu.Pr...]
    gather x3 -> x0, local copies, waits for them, and re-layouts: 6.65 us -> none  [the longest x1 2.22 us: shards(): along_y = jnp.take(shift_tables[1], positions[:, 1], axis=0)]
    squeeze x1 -> x0, local copies, waits for them, and re-layouts: 5.51 us -> none  [shards(): along_x = jnp.take(shift_tables[0], positions[:, 0], axis=0)]
    reduce_sum x2 -> x1, other arithmetic: 4.58 us -> 0.02 us  [shards(): absorbed = jnp.sum(absorbed, axis=0)]
    mul x1 -> x0, other arithmetic: 4.18 us -> none  [shards(): squares = widened * widened]
  transfers between devices with their start and end apart: 6 -> 6, of which waited for: 6 -> 6; matrix products, arithmetic and copies ran while one was open for 5% -> 7% of each run, Pallas kernels for 0% -> 0%
where the time goes in v1:
time: 124 us; the launch traced here: 123 us
  waiting for transfers between devices  52.5 us (42%)
  starting transfers between devices  36.2 us (29%)
  local copies, waits for them, and re-layouts  11.5 us (9%)
  Pallas kernels  11.3 us (9%)
  other arithmetic  8.57 us (7%)
  matrix products  2.23 us (2%)
    all_to_all x3, waiting for transfers between devices, from_everyone(): lax.all_to_all(jnp.broadcast_to(shard[None], (size, *shard.shape)), axis,...  31 us
    all_to_all x3, starting transfers between devices, from_everyone(): lax.all_to_all(jnp.broadcast_to(shard[None], (size, *shard.shape)), axis,...  14.7 us
    all_to_all x2, waiting for transfers between devices, sum_at_owner(): lax.all_to_all(parts, axis, split_axis=0, concat_axis=0, tiled=True)  12.5 us
    pallas_call x1, Pallas kernels, moved_sum(): pl.pallas_call(functools.partial(move_kernel, unroll), grid_spec=pltpu.Pr...  11.3 us
    all_to_all x2, starting transfers between devices, sum_at_owner(): lax.all_to_all(parts, axis, split_axis=0, concat_axis=0, tiled=True)  11.2 us
    all_to_all x1, starting transfers between devices, summed_rows(): lax.all_to_all(nearer, far, split_axis=0, concat_axis=0, tiled=True)  10.3 us
    all_to_all x1, waiting for transfers between devices, summed_rows(): lax.all_to_all(nearer, far, split_axis=0, concat_axis=0, tiled=True)  8.98 us
    div x60, other arithmetic, angular_basis(): pi_terms.append(azim_order * current / sine_theta)  3.65 us
  transfers between devices with their start and end apart: 6, of which 6 were waited for; matrix products, arithmetic and copies ran while one was open for 7% of the time, Pallas kernels for 0%

profile of v1, /device:TPU:1, one launch (start us, length us, event | category | flops | bytes accessed | tf_op | source)
XLA Modules:
  0.0 123.4 jit_solution(10563048136749747459)
XLA Ops:
  0.6 0.8 copy.28
  1.4 0.6 reshape.3830.cells_ref
  2.0 11.3 %move.1 = (f32[480,512]{1,0:T(8,128)}, f32[8,512]{1,0:T(8,128)}) custom-call(s32[24]{0:T(128)} %reshape.3830.cells_ref, bf16[8,240,1024]{2,1,0:T(8,128)(2,1)} %coef_ref.1, bf16[3,8,480,240]{3,2,1,0:T(8,128)(2,1)} %refs_5_.1, bf16[3,8,480,240]{3,2,1,0:T(8,128)(2,1)} %refs_5_.1, bf16[3,8,480,240]{3,2,1,0:T(8,128)(2,1)} %refs_5_.1, ...), custom_call_target="tpu_custom_call" | custom-call | flops 6000000000 | bytes 10000000 | tf_op jit(solution)/shard_map/move/pallas_call | solution.py:226
  13.3 1.3 %fusion.44 = (f32[240,512]{1,0:T(8,128)S(1)}, f32[512]{0:T(512)S(1)}, f32[240,512]{1,0:T(8,128)S(1)}) fusion(f32[480,512]{1,0:T(8,128)} %get-tuple-element.4, f32[240,1024]{1,0:T(8,128)S(1)} %copy-done), kind=kLoop, calls=%fused_computation.309 | loop fusion | flops 491008 | bytes 2951168 | tf_op jit(solution)/shard_map/slice | solution.py:260
  15.0 0.8 reshape_reshape.9
  15.9 1.6 %copy.29 = f32[8,32,964]{2,1,0:T(8,128)} copy(f32[8,32,964]{2,0,1:T(8,128)S(1)} %bitcast.47) | data formatting | bytes 1974272 | tf_op jit(solution)/shard_map/transpose | solution.py:23
  17.5 7.0 %all-to-all-start = ((f32[8,32,964]{2,1,0:T(8,128)}), f32[8,32,964]{2,1,0:T(8,128)S(1)}, u32[]{:S(2)}, u32[]{:S(2)}) async-start(f32[8,32,964]{2,1,0:T(8,128)} %copy.29), calls=%async_computation | async-start | bytes 2097152 | tf_op jit(solution)/shard_map/all_to_all | solution.py:28
  30.4 9.1 %all-to-all-done = f32[8,32,964]{2,1,0:T(8,128)S(1)} async-done(((f32[8,32,964]{2,1,0:T(8,128)}), f32[8,32,964]{2,1,0:T(8,128)S(1)}, u32[]{:S(2)}, u32[]{:S(2)}) %all-to-all-start) | async-done | bytes 987168 | tf_op jit(solution)/shard_map/all_to_all | solution.py:28
  39.6 0.7 all_to_all.27
  40.3 10.3 %all-to-all-start.1 = ((f32[32,1,964]{2,1,0:T(1,128)}), f32[32,1,964]{2,1,0:T(1,128)S(1)}, u32[]{:S(2)}, u32[]{:S(2)}) async-start(f32[32,1,964]{2,1,0:T(1,128)} %all_to_all.27), calls=%async_computation.1 | async-start | bytes 262144 | tf_op jit(solution)/shard_map/all_to_all | solution.py:36
  50.8 9.0 %all-to-all-done.1 = f32[32,1,964]{2,1,0:T(1,128)S(1)} async-done(((f32[32,1,964]{2,1,0:T(1,128)}), f32[32,1,964]{2,1,0:T(1,128)S(1)}, u32[]{:S(2)}, u32[]{:S(2)}) %all-to-all-start.1) | async-done | bytes 123424 | tf_op jit(solution)/shard_map/all_to_all | solution.py:36
  59.9 0.7 broadcast_in_dim.10
  60.6 3.9 %all-to-all-start.2 = ((f32[32,1,964]{2,1,0:T(1,128)}), f32[32,1,964]{2,1,0:T(1,128)S(1)}, u32[]{:S(2)}, u32[]{:S(2)}) async-start(f32[32,1,964]{2,1,0:T(1,128)} %broadcast_in_dim.10), calls=%async_computation.2 | async-start | bytes 262144 | tf_op jit(solution)/shard_map/all_to_all | solution.py:47
  64.5 0.2 stack.29
  64.8 0.3 stack.28
  65.1 8.5 %all-to-all-done.2 = f32[32,1,964]{2,1,0:T(1,128)S(1)} async-done(((f32[32,1,964]{2,1,0:T(1,128)}), f32[32,1,964]{2,1,0:T(1,128)S(1)}, u32[]{:S(2)}, u32[]{:S(2)}) %all-to-all-start.2) | async-done | bytes 123424 | tf_op jit(solution)/shard_map/all_to_all | solution.py:47
  73.6 1.1 broadcast_in_dim.12
  74.7 7.1 %all-to-all-start.3 = ((f32[8,32,964]{2,1,0:T(8,128)}), f32[8,32,964]{2,1,0:T(8,128)S(1)}, u32[]{:S(2)}, u32[]{:S(2)}) async-start(f32[8,32,964]{2,1,0:T(8,128)} %broadcast_in_dim.12), calls=%async_computation.3 | async-start | bytes 2097152 | tf_op jit(solution)/shard_map/all_to_all | solution.py:47
  82.2 14.6 %all-to-all-done.3 = f32[8,32,964]{2,1,0:T(8,128)S(1)} async-done(((f32[8,32,964]{2,1,0:T(8,128)}), f32[8,32,964]{2,1,0:T(8,128)S(1)}, u32[]{:S(2)}, u32[]{:S(2)}) %all-to-all-start.3) | async-done | bytes 987168 | tf_op jit(solution)/shard_map/all_to_all | solution.py:47
  96.8 0.6 copy.30
  97.4 1.2 slice.40
  98.6 0.7 fusion
  99.3 0.7 fusion.1
  100.2 0.8 convolution_bitcast_fusion
  101.0 4.2 %all-to-all-start.4 = ((f32[8,1,64]{2,1,0:T(1,128)}), f32[8,1,64]{2,1,0:T(1,128)S(1)}, u32[]{:S(2)}, u32[]{:S(2)}) async-start(f32[8,1,64]{2,1,0:T(1,128)} %convolution_bitcast_fusion), calls=%async_computation.4 | async-start | bytes 8192 | tf_op jit(solution)/shard_map/all_to_all | solution.py:28
  105.2 1.1 slice.46
  106.3 3.4 %all-to-all-done.4 = f32[8,1,64]{2,1,0:T(1,128)S(1)} async-done(((f32[8,1,64]{2,1,0:T(1,128)}), f32[8,1,64]{2,1,0:T(1,128)S(1)}, u32[]{:S(2)}, u32[]{:S(2)}) %all-to-all-start.4) | async-done | bytes 2080 | tf_op jit(solution)/shard_map/all_to_all | solution.py:28
  109.7 0.6 broadcast_in_dim.13
  110.3 3.8 %all-to-all-start.5 = ((f32[32,1,64]{2,1,0:T(1,128)}), f32[32,1,64]{2,1,0:T(1,128)S(1)}, u32[]{:S(2)}, u32[]{:S(2)}) async-start(f32[32,1,64]{2,1,0:T(1,128)} %broadcast_in_dim.13), calls=%async_computation.5 | async-start | bytes 32768 | tf_op jit(solution)/shard_map/all_to_all | solution.py:47
  114.2 0.7 copy.33
  114.9 7.9 %all-to-all-done.5 = f32[32,1,64]{2,1,0:T(1,128)S(1)} async-done(((f32[32,1,64]{2,1,0:T(1,128)}), f32[32,1,64]{2,1,0:T(1,128)S(1)}, u32[]{:S(2)}, u32[]{:S(2)}) %all-to-all-start.5) | async-done | bytes 8224 | tf_op jit(solution)/shard_map/all_to_all | solution.py:47
  122.8 0.6 pad_maximum_fusion.2
  (130 shorter events, 7.1 us)
Async XLA Ops:
  2.0 11.3 %copy-start = (f32[240,1024]{1,0:T(8,128)S(1)}, f32[240,1024]{1,0:T(8,128)}, u32[]{:S(2)}) copy-start(f32[240,1024]{1,0:T(8,128)} %param.13) | copy-start | bytes 2949124
  13.3 1.6 %copy-start.1 = (f32[8,512]{1,0:T(8,128)S(1)}, f32[8,512]{1,0:T(8,128)}, u32[]{:S(2)}) copy-start(f32[8,512]{1,0:T(8,128)} %get-tuple-element.5) | copy-start | bytes 49156
  15.9 65.9 %copy-start.3 = (f32[120]{0:T(128)S(1)}, f32[120]{0:T(128)}, u32[]{:S(2)}) copy-start(f32[120]{0:T(128)} %constant.607.clone) | copy-start | bytes 1444
  15.9 65.9 %copy-start.4 = (f32[120]{0:T(128)S(1)}, f32[120]{0:T(128)}, u32[]{:S(2)}) copy-start(f32[120]{0:T(128)} %constant.606.clone) | copy-start | bytes 1444
  15.9 65.9 %copy-start.5 = (f32[120]{0:T(128)S(1)}, f32[120]{0:T(128)}, u32[]{:S(2)}) copy-start(f32[120]{0:T(128)} %constant.605.clone) | copy-start | bytes 1444
  15.9 66.2 %copy-start.2 = (f32[4,64]{1,0:T(4,128)S(1)}, f32[4,64]{1,0:T(4,128)}, u32[]{:S(2)}) copy-start(f32[4,64]{1,0:T(4,128)} %param.14) | copy-start | bytes 3076
  17.5 22.0 %all-to-all-start = ((f32[8,32,964]{2,1,0:T(8,128)}), f32[8,32,964]{2,1,0:T(8,128)S(1)}, u32[]{:S(2)}, u32[]{:S(2)}) async-start(f32[8,32,964]{2,1,0:T(8,128)} %copy.29), calls=%async_computation | async-start | bytes 2097152 | tf_op jit(solution)/shard_map/all_to_all | solution.py:28
  40.3 19.5 %all-to-all-start.1 = ((f32[32,1,964]{2,1,0:T(1,128)}), f32[32,1,964]{2,1,0:T(1,128)S(1)}, u32[]{:S(2)}, u32[]{:S(2)}) async-start(f32[32,1,964]{2,1,0:T(1,128)} %all_to_all.27), calls=%async_computation.1 | async-start | bytes 262144 | tf_op jit(solution)/shard_map/all_to_all | solution.py:36
  60.6 13.0 %all-to-all-start.2 = ((f32[32,1,964]{2,1,0:T(1,128)}), f32[32,1,964]{2,1,0:T(1,128)S(1)}, u32[]{:S(2)}, u32[]{:S(2)}) async-start(f32[32,1,964]{2,1,0:T(1,128)} %broadcast_in_dim.10), calls=%async_computation.2 | async-start | bytes 262144 | tf_op jit(solution)/shard_map/all_to_all | solution.py:47
  74.7 22.1 %all-to-all-start.3 = ((f32[8,32,964]{2,1,0:T(8,128)}), f32[8,32,964]{2,1,0:T(8,128)S(1)}, u32[]{:S(2)}, u32[]{:S(2)}) async-start(f32[8,32,964]{2,1,0:T(8,128)} %broadcast_in_dim.12), calls=%async_computation.3 | async-start | bytes 2097152 | tf_op jit(solution)/shard_map/all_to_all | solution.py:47
  101.0 8.7 %all-to-all-start.4 = ((f32[8,1,64]{2,1,0:T(1,128)}), f32[8,1,64]{2,1,0:T(1,128)S(1)}, u32[]{:S(2)}, u32[]{:S(2)}) async-start(f32[8,1,64]{2,1,0:T(1,128)} %convolution_bitcast_fusion), calls=%async_computation.4 | async-start | bytes 8192 | tf_op jit(solution)/shard_map/all_to_all | solution.py:28
  110.3 12.5 %all-to-all-start.5 = ((f32[32,1,64]{2,1,0:T(1,128)}), f32[32,1,64]{2,1,0:T(1,128)S(1)}, u32[]{:S(2)}, u32[]{:S(2)}) async-start(f32[32,1,64]{2,1,0:T(1,128)} %broadcast_in_dim.13), calls=%async_computation.5 | async-start | bytes 32768 | tf_op jit(solution)/shard_map/all_to_all | solution.py:47

commit v2 on v0

v2 whole, which is shorter than its diff:
```python
import functools
import math

import jax
import jax.numpy as jnp
import numpy as np
from jax import lax
from jax.experimental import pallas as pl
from jax.experimental.pallas import tpu as pltpu
from jax.sharding import Mesh
from jax.sharding import PartitionSpec as P

ORDER = 10
AZIM = 64
POLAR = 128
COEFS = 240
HALF = 120
FIELDS = 512
ROWS = 256
CHUNK = 32
LANES = 128
SPH_ANG = ("sph_0", "sph_1", "ang_0", "ang_1")
SPH = ("sph_0", "sph_1")
ANG = ("ang_0", "ang_1")
PLANE = ("ang_0", "sph_0")
LINE = "sph_1"
PAIR = "ang_1"
F32 = jnp.float32
BF16 = jnp.bfloat16


def index_tables():
    degree, order = np.zeros(LANES), np.zeros(LANES)
    for n in range(1, ORDER + 1):
        for m in range(-n, n + 1):
            degree[n * n - 1 + n + m] = n
            order[n * n - 1 + n + m] = m
    size = np.abs(order)
    used = degree > 0
    rise, fall = np.zeros((ORDER + 1, LANES)), np.zeros((ORDER + 1, LANES))
    for t in range(1, ORDER + 1):
        on = used & (size < t) & (t <= degree)
        s = size[on]
        rise[t, on] = np.sqrt((4.0 * t * t - 1.0) / (t * t - s * s))
        if t > 1:
            fall[t, on] = np.sqrt(((t - 1.0) ** 2 - s * s) / (4.0 * (t - 1.0) ** 2 - 1.0))
    link = np.sqrt((2 * degree + 1) * (degree**2 - order**2) / np.maximum(2 * degree - 1, 1)) * used
    norm = used / np.sqrt(np.maximum(degree * (degree + 1.0), 1.0))
    unit = np.array([1.0, -1.0j, -1.0, 1.0j])[(degree.astype(int) + 1) % 4] * norm
    return degree, order, size, rise, fall, link, unit


def radial(cos_theta, sine_theta):
    degree, order, size, rise, fall, link, _ = index_tables()
    row = lambda v: jnp.asarray(np.asarray(v, np.float32)[None, :])
    current = jnp.full((cos_theta.shape[0], LANES), 1.0 / math.sqrt(4.0 * math.pi), F32)
    for t in range(1, ORDER + 1):
        factor = -math.sqrt((2.0 * t + 1.0) / (2.0 * t))
        current = jnp.where(row(size) >= t, factor * sine_theta * current, current)
    previous = jnp.zeros_like(current)
    for t in range(1, ORDER + 1):
        following = row(rise[t]) * (cos_theta * current - row(fall[t]) * previous)
        on = row(rise[t]) > 0
        previous, current = jnp.where(on, current, previous), jnp.where(on, following, current)
    pi_term = row(order) * current / sine_theta
    tau_term = (row(degree) * cos_theta * current - row(link) * previous) / sine_theta
    return jnp.stack([tau_term + pi_term, tau_term - pi_term])


def halves(value):
    high = value.astype(BF16)
    return high, (value - high.astype(F32)).astype(BF16)


def swap_chunks(blocks):
    group = lax.broadcasted_iota(jnp.int32, blocks[0].shape, 1) // CHUNK
    out = []
    for x in range(4):
        mixed = None
        for g in range(4):
            shift = (g - x) * CHUNK % LANES
            piece = pltpu.roll(blocks[g], shift, 1) if shift else blocks[g]
            mixed = piece if mixed is None else jnp.where(group == g, piece, mixed)
        out.append(mixed)
    return out


def call(body, outs, ins, name, flops=1, limit=16, **kw):
    size = sum(math.prod(a.shape) * a.dtype.itemsize for a in list(outs) + list(ins))
    return pl.pallas_call(
        body,
        out_shape=[jax.ShapeDtypeStruct(o.shape, o.dtype) for o in outs],
        compiler_params=pltpu.CompilerParams(vmem_limit_bytes=limit * 1024 * 1024),
        cost_estimate=pl.CostEstimate(flops=flops, bytes_accessed=size, transcendentals=0),
        name=name,
        **kw,
    )(*ins)


def struct(shape, dtype=F32):
    return jax.ShapeDtypeStruct(shape, dtype)


def move_kernel(
    unroll, scalar_ref, coef_hbm, table_hbm, weight_ref, mine_ref, theirs_ref,
    coef, table, total, absorbed, right, sems,
):
    spheres = coef.shape[0]
    groups = spheres // unroll

    def coef_copy(j):
        return pltpu.make_async_copy(coef_hbm.at[j], coef.at[j], sems.at[3, j])

    def table_copy(j, stage):
        axis = 2 - stage
        cell = scalar_ref[1 + 3 * j + axis]
        return pltpu.make_async_copy(
            table_hbm.at[axis, cell], table.at[stage, j], sems.at[stage, j]
        )

    def fetches(group):
        own = range(group * unroll, (group + 1) * unroll)
        first = [copy for j in own for copy in (coef_copy(j), table_copy(j, 0))]
        return first, [table_copy(j, stage) for stage in (1, 2) for j in own]

    first, second = fetches(0)
    for copy in first + second:
        copy.start()
    total[...] = jnp.zeros_like(total)
    absorbed[...] = jnp.zeros_like(absorbed)
    weights = weight_ref[...].T
    for group in range(groups):
        if group + 1 < groups:
            ahead = fetches(group + 1)
            for copy in ahead[0] + ahead[1]:
                copy.start()
        for copy in first if group == 0 else first + second:
            copy.wait()
        for s in range(unroll):
            j = group * unroll + s
            real, imag = coef[j, :, :FIELDS].astype(F32), coef[j, :, FIELDS:].astype(F32)
            energy = (real * real + imag * imag) * weights[:, j : j + 1]
            absorbed[...] += jnp.sum(energy.reshape(COEFS // 8, 8, FIELDS), axis=0)
        for stage in range(3):
            if group == 0 and stage == 1:
                for copy in second:
                    copy.wait()
            for s in range(unroll):
                j = group * unroll + s
                matrix = table[stage, j]
                turned = jnp.concatenate([-matrix[COEFS:], matrix[:COEFS]], axis=0)
                if stage == 0:
                    real, imag = coef[j, :, :FIELDS], coef[j, :, FIELDS:]
                else:
                    real, imag = right[s, :COEFS], right[s, ROWS : ROWS + COEFS]
                product = jnp.dot(matrix, real, preferred_element_type=F32) + jnp.dot(
                    turned, imag, preferred_element_type=F32
                )
                if stage < 2:
                    product = product.astype(BF16)
                    right[s, :COEFS] = product[:COEFS]
                    right[s, ROWS : ROWS + COEFS] = product[COEFS:]
                else:
                    total[0, :COEFS] += product[:COEFS]
                    total[1, :COEFS] += product[COEFS:]
        if group + 1 < groups:
            first, second = ahead
    total[0, COEFS : COEFS + 1] = jnp.sum(absorbed[...], axis=0, keepdims=True)
    core = scalar_ref[0]
    mine_ref[...] = total[core]
    theirs_ref[...] = total[1 - core]


def moved_sum(coefficients, positions, shift_tables, absorb_weight, core, unroll=2):
    spheres = coefficients.shape[0]
    scalars = jnp.concatenate([core.reshape(1), positions.reshape(-1)])
    hbm = pl.BlockSpec(memory_space=pltpu.HBM)
    vmem = pl.BlockSpec(memory_space=pltpu.VMEM)
    return pl.pallas_call(
        functools.partial(move_kernel, unroll),
        in_specs=[pl.BlockSpec(memory_space=pltpu.SMEM), hbm, hbm, vmem],
        out_specs=[vmem, vmem],
        scratch_shapes=[
            pltpu.VMEM((spheres, COEFS, 2 * FIELDS), BF16),
            pltpu.VMEM((3, spheres, 2 * COEFS, COEFS), BF16),
            pltpu.VMEM((2, ROWS, FIELDS), F32),
            pltpu.VMEM((8, FIELDS), F32),
            pltpu.VMEM((unroll, 2 * ROWS, FIELDS), BF16),
            pltpu.SemaphoreType.DMA((4, spheres)),
        ],
        out_shape=[struct((ROWS, FIELDS))] * 2,
        compiler_params=pltpu.CompilerParams(vmem_limit_bytes=62 * 1024 * 1024),
        cost_estimate=pl.CostEstimate(
            flops=6_000_000_000, bytes_accessed=10_000_000, transcendentals=0
        ),
        name="move",
    )(scalars, coefficients, shift_tables, absorb_weight)


def pack_kernel(mine_ref, other_ref, detector_ref, out_ref):
    detector = detector_ref[...]
    detector = jnp.concatenate([detector[:, :CHUNK], detector[:, CHUNK:]], axis=0)
    for tile in range(4):
        lanes = slice(tile * LANES, (tile + 1) * LANES)
        blocks = [
            mine_ref[g * 64 : (g + 1) * 64, lanes] + other_ref[g * 64 : (g + 1) * 64, lanes]
            for g in range(4)
        ]
        for x, block in enumerate(swap_chunks(blocks)):
            out_ref[4 * tile + x] = block
            out_ref[4 * tile + x, 56:, 96:] = detector


def plane_kernel(got_ref, out_ref):
    total = got_ref[0]
    for k in range(1, 16):
        total = total + got_ref[k]
    group = lax.broadcasted_iota(jnp.int32, (8, LANES), 1) // CHUNK
    detectors = got_ref[3, 56:]
    for x in range(3):
        detectors = jnp.where(
            group == x, pltpu.roll(got_ref[x, 56:], (x + 1) * CHUNK, 1), detectors
        )
    for k in range(8):
        out_ref[k, :64] = total
        out_ref[k, 64:] = detectors


def basis_kernel(radial_ref, cos_ref, sin_ref, high_ref, low_ref):
    for sign in range(2):
        for trig, ref in enumerate((cos_ref, sin_ref)):
            block = radial_ref[sign][None, :, None, :] * ref[...].reshape(4, 1, 8, LANES)
            high, low = halves(block.reshape(2 * ROWS, LANES))
            lanes = slice((2 * sign + trig) * LANES, (2 * sign + trig + 1) * LANES)
            high_ref[:, lanes] = high
            low_ref[:, lanes] = low


def power_kernel(radial_ref, scaled_ref, line_ref, waves_ref, gap_ref, out_ref):
    gap = gap_ref[...]
    far = jnp.abs(gap)
    far = jnp.concatenate([far, far], axis=1)
    detectors = line_ref[:, 64:].reshape(64, LANES)
    group = lax.broadcasted_iota(jnp.int32, detectors.shape, 1) // CHUNK
    detectors = jnp.concatenate([jnp.where(group == x, detectors, 0.0) for x in range(4)], axis=0)
    spectrum = jnp.dot(
        detectors, waves_ref[...], preferred_element_type=F32, precision=lax.Precision.HIGHEST
    )
    spectrum = spectrum[:, :LANES] + pltpu.roll(spectrum[:, LANES:], 2 * LANES - 4, 0)
    spectrum = jnp.concatenate([spectrum[8 * k : 8 * k + 4] for k in range(32)], axis=0)
    for sign in range(2):
        table = scaled_ref[sign]
        left_high, left_low = halves(radial_ref[sign].T)
        left = jnp.concatenate([left_high, left_high], axis=1)
        total = jnp.zeros((LANES, 2 * LANES), F32)
        for d in range(2 * ORDER + 1):
            right = jnp.concatenate(
                [table * spectrum[:, d : d + 1], table * spectrum[:, 64 + d : 65 + d]], axis=1
            )
            high, low = halves(right)
            product = jnp.dot(
                left, jnp.concatenate([high, low], axis=0), preferred_element_type=F32
            ) + jnp.dot(left_low, high, preferred_element_type=F32)
            total = jnp.where(far == d, product, total)
        out_ref[sign, :, :LANES] = total[:, :LANES]
        out_ref[sign, :, LANES:] = jnp.where(gap < 0, -total[:, LANES:], total[:, LANES:])


def spread_rows(packed):
    parts = [packed] + [pltpu.roll(packed, LANES - g * CHUNK, 1) for g in (1, 2, 3)]
    return jnp.concatenate(parts, axis=0)


def columns(group, pieces):
    out = pieces[0]
    for g in (1, 2, 3):
        out = jnp.where(group == g, pltpu.roll(pieces[g], g * CHUNK, 1), out)
    return out


def far_kernel(
    core_ref, own_ref, other_ref, high_ref, low_ref, form_ref, phase_ref,
    incident_ref, incident_imag_ref, out_ref,
):
    core = core_ref[0]
    own, other = own_ref[...], other_ref[...]
    real = spread_rows(jnp.where(core == 0, own, other))
    imag = spread_rows(jnp.where(core == 0, other, own))
    group = lax.broadcasted_iota(jnp.int32, (HALF, LANES), 1) // CHUNK
    spare = jnp.zeros((8, LANES), F32)
    phase_real, phase_imag = phase_ref[0], phase_ref[1]
    real_1, real_2 = real[:HALF], real[HALF:COEFS]
    imag_1, imag_2 = imag[:HALF], imag[HALF:COEFS]
    rows = []
    collected = jnp.zeros((1, LANES), F32)
    for sign in range(2):
        if sign == 0:
            both = (real_2 - imag_1, imag_2 + real_1)
        else:
            both = (real_2 + imag_1, imag_2 - real_1)
        re = phase_real * both[0] - phase_imag * both[1]
        im = phase_real * both[1] + phase_imag * both[0]
        if sign == 0:
            top = columns(group, (re, im, -im, re))
            low = columns(group, (-im, re, -re, -im))
        else:
            top = columns(group, (re, im, im, -re))
            low = columns(group, (-im, re, re, im))
        rows += [0.5 * top, spare, 0.5 * low, spare]
        pair = jnp.concatenate([jnp.where(group == 0, re, 0.0), spare], axis=0)
        pair_imag = jnp.concatenate([jnp.where(group == 0, im, 0.0), spare], axis=0)
        dot = functools.partial(
            jnp.dot, preferred_element_type=F32, precision=lax.Precision.HIGHEST
        )
        even, odd = form_ref[sign, :, :LANES], form_ref[sign, :, LANES:]
        collected += 0.5 * jnp.sum(
            pair * dot(even, pair)
            + pair_imag * (dot(even, pair_imag) + 2.0 * dot(odd, pair)),
            axis=0,
            keepdims=True,
        )
    high, low = halves(jnp.concatenate(rows, axis=0))
    wide = jnp.dot(
        high_ref[...], jnp.concatenate([high, low], axis=1), preferred_element_type=F32
    )
    result = (
        wide[:, :LANES]
        + wide[:, LANES:]
        + jnp.dot(low_ref[...], high, preferred_element_type=F32)
    )
    extinction = jnp.sum(
        incident_ref[...] * real[:COEFS, :CHUNK] + incident_imag_ref[...] * imag[:COEFS, :CHUNK],
        axis=0,
        keepdims=True,
    )
    stats = jnp.concatenate(
        [
            extinction,
            real[COEFS : COEFS + 1, :CHUNK],
            collected[:, :CHUNK],
            jnp.zeros((1, CHUNK), F32),
        ],
        axis=1,
    )
    stats = jnp.broadcast_to(stats, (8, LANES))
    for k in range(16):
        out_ref[k, :CHUNK] = result[k * CHUNK : (k + 1) * CHUNK]
        out_ref[k, CHUNK:] = stats


def finish_kernel(place_ref, got_ref, amplitude_ref, stats_ref):
    for tile in range(4):
        blocks = [got_ref[4 * tile + x, :CHUNK] for x in range(4)]
        for q, block in enumerate(swap_chunks(blocks)):
            amplitude_ref[q, :, tile * LANES : (tile + 1) * LANES] = block
    place = place_ref[0]
    first = got_ref[place, CHUNK : CHUNK + 1]
    second = got_ref[place + 1, CHUNK : CHUNK + 1]
    stats_ref[...] = jnp.concatenate(
        [
            jnp.concatenate(
                [v[:, r * CHUNK : (r + 1) * CHUNK] for v in (first, second)], axis=1
            )
            for r in range(3)
        ],
        axis=0,
    )


def shards(coefficients, positions, shift_tables, absorb_weight, incident, detector):
    x, z = lax.axis_index("sph_0"), lax.axis_index("sph_1")
    y, core = lax.axis_index("ang_0"), lax.axis_index("ang_1")
    smem = pl.BlockSpec(memory_space=pltpu.SMEM)
    vmem = pl.BlockSpec(memory_space=pltpu.VMEM)

    mine, theirs = moved_sum(
        coefficients, positions, shift_tables, absorb_weight, core.astype(jnp.int32)
    )
    other = lax.ppermute(theirs, PAIR, [(0, 1), (1, 0)])
    (packed,) = call(pack_kernel, [struct((16, 64, LANES))], [mine, other, detector], "pack")
    packed, incident, z, y, core, polar = lax.optimization_barrier(
        (packed, incident, z, y, core, jnp.arange(POLAR))
    )
    (spread,) = call(
        plane_kernel,
        [struct((8, 72, LANES))],
        [lax.all_to_all(packed, PLANE, 0, 0, tiled=True)],
        "plane",
    )
    line = lax.all_to_all(spread, LINE, 0, 0, tiled=True)
    own = line[:, :64].sum(axis=0)
    partner = lax.ppermute(own, PAIR, [(0, 1), (1, 0)])

    degree, order, size, rise, fall, link, unit = index_tables()
    theta = (polar.astype(F32) + 0.5) * (math.pi / POLAR)
    cos_theta, sine_theta = jnp.cos(theta)[:, None], jnp.sin(theta)[:, None]
    whole = radial(cos_theta, sine_theta)
    solid_angle = 2.0 * math.pi * math.pi / (POLAR * AZIM)
    scaled = whole * (sine_theta * solid_angle)
    near_polar = ((jnp.arange(4) * 8 + z)[:, None] * 4 + jnp.arange(4)[None, :]).reshape(-1)
    near_theta = (near_polar.astype(F32) + 0.5) * (math.pi / POLAR)
    near = radial(jnp.cos(near_theta)[:, None], jnp.sin(near_theta)[:, None])
    near_azim = ((jnp.arange(4) * 2 + core)[:, None] * 8 + jnp.arange(8)[None, :]).reshape(-1)
    azimuth = near_azim.astype(F32) * (2.0 * math.pi / AZIM)
    angle = azimuth[:, None] * jnp.asarray(np.asarray(order, np.float32))[None, :]
    high, low = call(
        basis_kernel,
        [struct((2 * ROWS, 2 * ROWS), BF16)] * 2,
        [near, jnp.cos(angle), jnp.sin(angle)],
        "basis",
        flops=10_000_000,
    )
    turns = np.arange(AZIM)[:, None] * np.arange(2 * ORDER + 1)[None, :] % AZIM
    waves = np.zeros((AZIM, LANES), np.float32)
    waves[:, : 2 * ORDER + 1] = np.cos(2.0 * math.pi * turns / AZIM)
    waves[:, 64 : 64 + 2 * ORDER + 1] = np.sin(2.0 * math.pi * turns / AZIM)
    waves = np.tile(np.concatenate([waves[:CHUNK], waves[CHUNK:]], axis=1), (4, 1))
    gap = np.where((degree[:, None] > 0) & (degree[None, :] > 0), order[None, :] - order[:, None], 99)
    (form,) = call(
        power_kernel,
        [struct((2, LANES, 2 * LANES))],
        [whole, scaled, line, jnp.asarray(waves), jnp.asarray(gap.astype(np.int32))],
        "power",
        flops=1_000_000_000,
    )
    first = (4 * y + x) * CHUNK
    phase = np.stack([unit.real[:HALF], unit.imag[:HALF]]).astype(np.float32)
    phase = jnp.asarray(np.broadcast_to(phase[:, :, None], (2, HALF, LANES)))
    (messages,) = call(
        far_kernel,
        [struct((16, 40, LANES))],
        [
            core.astype(jnp.int32).reshape(1), own, partner, high, low, form, phase,
            lax.dynamic_slice_in_dim(incident, first, CHUNK, 1),
            lax.dynamic_slice_in_dim(incident, FIELDS + first, CHUNK, 1),
        ],
        "far",
        flops=400_000_000,
        in_specs=[smem] + [vmem] * 8,
    )
    got = lax.all_to_all(messages, PLANE, 0, 0, tiled=True)
    amplitude, stats = call(
        finish_kernel,
        [struct((4, 32, FIELDS)), struct((3, 64))],
        [(4 * y + 2 * core).astype(jnp.int32).reshape(1), got],
        "finish",
        in_specs=[smem, vmem],
    )
    return (amplitude.reshape(2, 2, 4, 8, FIELDS), stats)


def solution(mesh):
    torus = Mesh(mesh.devices.reshape(4, 8, 4, 2), SPH_ANG)
    in_specs = (P(SPH_ANG, None, None), P(SPH_ANG, None), P(), P(SPH_ANG, None), P(), P(SPH, None))
    out_specs = (P(None, None, SPH, ANG, None), P(None, ANG))
    return jax.shard_map(
        shards, mesh=torus, in_specs=in_specs, out_specs=out_specs, check_vma=False
    )
```

time: 191 us -> 78 us (0.41)
  other arithmetic: 46.2 us -> 5.37 us
  matrix products: 32.3 us -> 0 us
  waiting for transfers between devices: 52.4 us -> 25 us
  local copies, waits for them, and re-layouts: 22.3 us -> 3.57 us
  Pallas kernels: 0 us -> 18.1 us
  starting transfers between devices: 35.8 us -> 24.2 us
    dot_general x7 -> x0, matrix products: 32.3 us -> none  [the longest x3 29.7 us: rotate_step(): jnp.einsum('sap,spf->saf', matrix, vector, preferred_element_type=jnp.flo...]
    all_to_all x6 -> x3, waiting for transfers between devices: 52.4 us -> 23.2 us  [the longest x1 8.94 us: shards(): got = lax.all_to_all(messages, PLANE, 0, 0, tiled=True)]
    all_to_all x6 -> x3, starting transfers between devices: 35.8 us -> 17 us  [the longest x1 8.36 us: shards(): line = lax.all_to_all(spread, LINE, 0, 0, tiled=True)]
    another operation x5 -> x1, other arithmetic: 18.4 us -> 0.01 us  [radial(): return jnp.stack([tau_term + pi_term, tau_term - pi_term])]
    pallas_call x0 -> x7, Pallas kernels: none -> 18.1 us  [the longest x1 10.4 us: moved_sum(): pl.pallas_call(functools.partial(move_kernel, unroll), in_specs=[pl.Block...]
    sub x1 -> x2, other arithmetic: 11.3 us -> 2.14 us  [radial(): return jnp.stack([tau_term + pi_term, tau_term - pi_term])]
    ppermute x0 -> x2, starting transfers between devices: none -> 7.28 us  [the longest x1 4 us: shards(): partner = lax.ppermute(own, PAIR, [(0, 1), (1, 0)])]
    gather x3 -> x0, local copies, waits for them, and re-layouts: 6.65 us -> none  [the longest x1 2.22 us: shards(): along_y = jnp.take(shift_tables[1], positions[:, 1], axis=0)]
  transfers between devices with their start and end apart: 6 -> 5, of which waited for: 6 -> 4; matrix products, arithmetic and copies ran while one was open for 5% -> 7% of each run, Pallas kernels for 0% -> 4%
where the time goes in v2:
time: 78 us; the launch traced here: 77.5 us
  waiting for transfers between devices  25 us (32%)
  starting transfers between devices  24.2 us (31%)
  Pallas kernels  18.1 us (23%)
  other arithmetic  5.37 us (7%)
  local copies, waits for them, and re-layouts  3.57 us (5%)
  between operations  1.34 us (2%)
    pallas_call x1, Pallas kernels, moved_sum(): pl.pallas_call(functools.partial(move_kernel, unroll), in_specs=[pl.Block...  10.4 us
    all_to_all x1, waiting for transfers between devices, shards(): got = lax.all_to_all(messages, PLANE, 0, 0, tiled=True)  8.94 us
    all_to_all x1, starting transfers between devices, shards(): line = lax.all_to_all(spread, LINE, 0, 0, tiled=True)  8.36 us
    all_to_all x1, waiting for transfers between devices, shards(): line = lax.all_to_all(spread, LINE, 0, 0, tiled=True)  8.28 us
    pallas_call x6, Pallas kernels, call(): pl.pallas_call(body, out_shape=[jax.ShapeDtypeStruct(o.shape, o.dtype) fo...  7.6 us
    all_to_all x1, waiting for transfers between devices, shards(): lax.all_to_all(packed, PLANE, 0, 0, tiled=True)  6 us
    all_to_all x1, starting transfers between devices, shards(): lax.all_to_all(packed, PLANE, 0, 0, tiled=True)  5.06 us
    ppermute x1, starting transfers between devices, shards(): partner = lax.ppermute(own, PAIR, [(0, 1), (1, 0)])  4 us
  transfers between devices with their start and end apart: 5, of which 4 were waited for; matrix products, arithmetic and copies ran while one was open for 7% of the time, Pallas kernels for 4%

profile of v2, /device:TPU:1, one launch (start us, length us, event | category | flops | bytes accessed | tf_op | source)
XLA Modules:
  0.0 77.5 jit_solution(9438824353712616049)
XLA Ops:
  0.6 0.8 copy.99
  1.4 0.1 reshape.7400
  1.5 0.6 pad_add_fusion.scalar_ref
  2.5 10.4 %move.1 = (f32[256,512]{1,0:T(8,128)}, f32[256,512]{1,0:T(8,128)}) custom-call(s32[25]{0:T(128)} %pad_add_fusion.scalar_ref, bf16[8,240,1024]{2,1,0:T(8,128)(2,1)} %coef_hbm.1, bf16[3,8,480,240]{3,2,1,0:T(8,128)(2,1)} %table_hbm.1, f32[8,240]{1,0:T(8,128)} %weight_ref.1), custom_call_target="tpu_custom_call" | custom-call | flops 6000000000 | bytes 10000000 | tf_op jit(solution)/shard_map/move/pallas_call | solution.py:179
  13.0 3.3 %collective-permute-start = (f32[256,512]{1,0:T(8,128)}, f32[256,512]{1,0:T(8,128)S(1)}, u32[]{:S(2)}, u32[]{:S(2)}) collective-permute-start(f32[256,512]{1,0:T(8,128)} %get-tuple-element.15), channel_id=1, source_target_pairs={{0,1},{1,0},{2,3},{3,2},{4,5},{5,4},{6,7},{7,6},{8,9},{9,8},{10,11... | collective-permute-start | bytes 1572872 | tf_op jit(solution)/shard_map/ppermute | solution.py:379
  16.2 1.7 %collective-permute-done.other_ref = f32[256,512]{1,0:T(8,128)S(1)} collective-permute-done((f32[256,512]{1,0:T(8,128)}, f32[256,512]{1,0:T(8,128)S(1)}, u32[]{:S(2)}, u32[]{:S(2)}) %collective-permute-start) | collective-permute-done | bytes 524320 | tf_op jit(solution)/shard_map/ppermute | solution.py:379
  18.0 1.0 %copy-done = f32[256,512]{1,0:T(8,128)S(1)} copy-done((f32[256,512]{1,0:T(8,128)S(1)}, f32[256,512]{1,0:T(8,128)}, u32[]{:S(2)}) %copy-start) | copy-done | bytes 524312
  19.0 1.3 %pack.1 = f32[16,64,128]{2,1,0:T(8,128)} custom-call(f32[256,512]{1,0:T(8,128)S(1)} %copy-done, f32[256,512]{1,0:T(8,128)S(1)} %collective-permute-done.other_ref, f32[4,64]{1,0:T(4,128)S(1)} %copy-done.1), custom_call_target="tpu_custom_call" | custom-call | flops 1 | bytes 1573888 | tf_op jit(solution)/shard_map/pack/pallas_call | solution.py:90
  20.4 0.1 mul.2085
  20.5 0.1 fusion.2
  20.6 0.1 reshape.7404
  20.7 0.1 reshape.7405
  20.8 5.1 %all-to-all-start = ((f32[16,64,128]{2,1,0:T(8,128)}), f32[16,64,128]{2,1,0:T(8,128)S(1)}, u32[]{:S(2)}, u32[]{:S(2)}) async-start(f32[16,64,128]{2,1,0:T(8,128)} %pack.1), calls=%async_computation | async-start | bytes 1048576 | tf_op jit(solution)/shard_map/all_to_all | solution.py:387
  25.9 0.1 multiply_sine_fusion
  26.4 1.0 %fusion.6 = f32[1,16,128]{2,1,0:T(8,128)S(1)} fusion(f32[16]{0:T(128)S(1)} %reshape.7405, f32[128]{0:T(128)S(1)} %copy-done.6, f32[128]{0:T(128)S(1)} %copy-done.7, f32[128]{0:T(128)S(1)} %copy-done.8, f32[128]{0:T(128)S(1)} %copy-done.9, f32[128]{0:T(128)S(1)} %copy-done.10, f32[128]{0:T(128)S(1)} %copy-done.11, f32[128]{0:T(128)S(1)} %copy-done.12, ...), kind=kLoop, calls=%fused_computation.97 | loop fusion | flops 174080 | bytes 22784 | tf_op jit(solution)/shard_map/sub | solution.py:67
  27.4 1.1 %constant_dynamic-slice_fusion = (f32[240,32]{1,0:T(8,128)S(1)}, f32[240,32]{1,0:T(8,128)S(1)}) fusion(f32[240,1024]{1,0:T(8,128)} %param.100, s32[]{:T(128)S(6)} %select_n.909, s32[]{:T(128)S(6)} %select_n.908), kind=kLoop, calls=%fused_computation.69 | loop fusion | bytes 122888 | tf_op jit(solution)/shard_map/dynamic_slice | solution.py:435
  28.5 1.0 %fusion.7 = f32[1,16,128]{2,1,0:T(8,128)S(1)} fusion(f32[16]{0:T(128)S(1)} %reshape.7405, f32[128]{0:T(128)S(1)} %copy-done.6, f32[128]{0:T(128)S(1)} %copy-done.7, f32[128]{0:T(128)S(1)} %copy-done.8, f32[128]{0:T(128)S(1)} %copy-done.9, f32[128]{0:T(128)S(1)} %copy-done.10, f32[128]{0:T(128)S(1)} %copy-done.11, f32[128]{0:T(128)S(1)} %copy-done.12, ...), kind=kLoop, calls=%fused_computation.98 | loop fusion | flops 174080 | bytes 22784 | tf_op jit(solution)/shard_map/add | solution.py:67
  29.5 1.2 %fusion.8 = f32[1,128,128]{2,1,0:T(8,128)S(1)} fusion(f32[128]{0:T(128)S(1)} %get-tuple-element.27, f32[128]{0:T(128)S(1)} %copy-done.6, f32[128]{0:T(128)S(1)} %copy-done.7, f32[128]{0:T(128)S(1)} %copy-done.8, f32[128]{0:T(128)S(1)} %copy-done.9, f32[128]{0:T(128)S(1)} %copy-done.10, f32[128]{0:T(128)S(1)} %copy-done.11, f32[128]{0:T(128)S(1)} %copy-done.12, ...), kind=kLoop, calls=%fused_computation.99 | loop fusion | flops 1392640 | bytes 85504 | tf_op jit(solution)/shard_map/sub | solution.py:67
  30.6 6.0 %all-to-all-done.got_ref = f32[16,64,128]{2,1,0:T(8,128)S(1)} async-done(((f32[16,64,128]{2,1,0:T(8,128)}), f32[16,64,128]{2,1,0:T(8,128)S(1)}, u32[]{:S(2)}, u32[]{:S(2)}) %all-to-all-start) | async-done | bytes 524320 | tf_op jit(solution)/shard_map/all_to_all | solution.py:387
  36.6 0.8 %plane.1 = f32[8,72,128]{2,1,0:T(8,128)} custom-call(f32[16,64,128]{2,1,0:T(8,128)S(1)} %all-to-all-done.got_ref), custom_call_target="tpu_custom_call" | custom-call | flops 1 | bytes 819200 | tf_op jit(solution)/shard_map/plane/pallas_call | solution.py:90
  37.4 8.4 %all-to-all-start.1 = ((f32[8,72,128]{2,1,0:T(8,128)}), f32[8,72,128]{2,1,0:T(8,128)S(1)}, u32[]{:S(2)}, u32[]{:S(2)}) async-start(f32[8,72,128]{2,1,0:T(8,128)} %plane.1), calls=%async_computation.1 | async-start | bytes 589824 | tf_op jit(solution)/shard_map/all_to_all | solution.py:390
  45.8 0.2 basis.1
  46.0 1.2 %fusion.9 = f32[1,128,128]{2,1,0:T(8,128)S(1)} fusion(f32[128]{0:T(128)S(1)} %get-tuple-element.27, f32[128]{0:T(128)S(1)} %copy-done.6, f32[128]{0:T(128)S(1)} %copy-done.7, f32[128]{0:T(128)S(1)} %copy-done.8, f32[128]{0:T(128)S(1)} %copy-done.9, f32[128]{0:T(128)S(1)} %copy-done.10, f32[128]{0:T(128)S(1)} %copy-done.11, f32[128]{0:T(128)S(1)} %copy-done.12, ...), kind=kLoop, calls=%fused_computation.100 | loop fusion | flops 1392640 | bytes 85504 | tf_op jit(solution)/shard_map/add | solution.py:67
  47.2 0.1 broadcast_multiply_fusion
  47.3 8.3 %all-to-all-done.1.line_ref = f32[8,72,128]{2,1,0:T(8,128)S(1)} async-done(((f32[8,72,128]{2,1,0:T(8,128)}), f32[8,72,128]{2,1,0:T(8,128)S(1)}, u32[]{:S(2)}, u32[]{:S(2)}) %all-to-all-start.1) | async-done | bytes 294944 | tf_op jit(solution)/shard_map/all_to_all | solution.py:390
  55.6 4.0 %collective-permute-start.1 = (f32[64,128]{1,0:T(8,128)S(1)}, f32[64,128]{1,0:T(8,128)S(1)}, u32[]{:S(2)}, u32[]{:S(2)}) collective-permute-start(f32[64,128]{1,0:T(8,128)S(1)} %slice_reduce_fusion.own_ref), channel_id=1, source_target_pairs={{0,1},{1,0},{2,3},{3,2},{4,5},{5,4},{6,7},{7,6},{8,9},{9,8},{10,11... | collective-permute-start | bytes 98312 | tf_op jit(solution)/shard_map/ppermute | solution.py:392
  59.6 2.7 %power.1.form_ref = f32[2,128,256]{2,1,0:T(8,128)S(1)} custom-call(f32[2,128,128]{2,1,0:T(8,128)S(1)} %get-tuple-element.31.radial_ref, f32[2,128,128]{2,1,0:T(8,128)S(1)} %get-tuple-element.30.scaled_ref, f32[8,72,128]{2,1,0:T(8,128)S(1)} %all-to-all-done.1.line_ref, f32[128,256]{1,0:T(8,128)S(1)} %copy-done.2, s32[128,128]{1,0:T(8,128)S(1)} %copy-done.3), custom_call_target="tpu_custom_call" | custom-call | flops 1000000000 | bytes 1015808 | tf_op jit(solution)/shard_map/power/pallas_call | solution.py:90
  62.3 0.1 jit_solution_.3.phase_ref
  62.4 1.6 %far.1 = f32[16,40,128]{2,1,0:T(8,128)} custom-call(s32[1]{0:T(128)} %bitcast.2.core_ref, f32[64,128]{1,0:T(8,128)S(1)} %slice_reduce_fusion.own_ref, f32[64,128]{1,0:T(8,128)S(1)} %collective-permute-done.1.other_ref, bf16[512,512]{1,0:T(8,128)(2,1)S(1)} %get-tuple-element.20.high_ref, bf16[512,512]{1,0:T(8,128)(2,1)S(1)} %get-tuple-element.21.low_ref, ...), custom_call_target="tpu_custom_call" | custom-call | flops 400000000 | bytes 1888260 | tf_op jit(solution)/shard_map/far/pallas_call | solution.py:90
  64.1 3.5 %all-to-all-start.2 = ((f32[16,40,128]{2,1,0:T(8,128)}), f32[16,40,128]{2,1,0:T(8,128)S(1)}, u32[]{:S(2)}, u32[]{:S(2)}) async-start(f32[16,40,128]{2,1,0:T(8,128)} %far.1), calls=%async_computation.2 | async-start | bytes 655360 | tf_op jit(solution)/shard_map/all_to_all | solution.py:441
  67.6 8.9 %all-to-all-done.2.got_ref = f32[16,40,128]{2,1,0:T(8,128)S(1)} async-done(((f32[16,40,128]{2,1,0:T(8,128)}), f32[16,40,128]{2,1,0:T(8,128)S(1)}, u32[]{:S(2)}, u32[]{:S(2)}) %all-to-all-start.2) | async-done | bytes 327712 | tf_op jit(solution)/shard_map/all_to_all | solution.py:441
  76.6 1.0 %finish.1 = (f32[4,32,512]{2,1,0:T(8,128)}, f32[3,64]{1,0:T(4,128)}) custom-call(s32[1]{0:T(128)} %bitcast.1.place_ref, f32[16,40,128]{2,1,0:T(8,128)S(1)} %all-to-all-done.2.got_ref), custom_call_target="tpu_custom_call" | custom-call | flops 1 | bytes 590596 | tf_op jit(solution)/shard_map/finish/pallas_call | solution.py:90
  (90 shorter events, 0.4 us)
Async XLA Ops:
  2.1 24.0 %copy-start.5 = (f32[128]{0:T(128)S(1)}, f32[128]{0:T(128)}, u32[]{:S(2)}) copy-start(f32[128]{0:T(128)} %constant.254) | copy-start | bytes 1540
  2.1 24.0 %copy-start.6 = (f32[128]{0:T(128)S(1)}, f32[128]{0:T(128)}, u32[]{:S(2)}) copy-start(f32[128]{0:T(128)} %constant.253) | copy-start | bytes 1540
  2.1 24.0 %copy-start.7 = (f32[128]{0:T(128)S(1)}, f32[128]{0:T(128)}, u32[]{:S(2)}) copy-start(f32[128]{0:T(128)} %constant.252) | copy-start | bytes 1540
  2.1 24.0 %copy-start.8 = (f32[128]{0:T(128)S(1)}, f32[128]{0:T(128)}, u32[]{:S(2)}) copy-start(f32[128]{0:T(128)} %constant.251) | copy-start | bytes 1540
  2.1 24.0 %copy-start.9 = (f32[128]{0:T(128)S(1)}, f32[128]{0:T(128)}, u32[]{:S(2)}) copy-start(f32[128]{0:T(128)} %constant.250) | copy-start | bytes 1540
  2.1 24.0 %copy-start.10 = (f32[128]{0:T(128)S(1)}, f32[128]{0:T(128)}, u32[]{:S(2)}) copy-start(f32[128]{0:T(128)} %constant.249) | copy-start | bytes 1540
  2.1 24.0 %copy-start.11 = (f32[128]{0:T(128)S(1)}, f32[128]{0:T(128)}, u32[]{:S(2)}) copy-start(f32[128]{0:T(128)} %constant.248) | copy-start | bytes 1540
  2.1 24.0 %copy-start.12 = (f32[128]{0:T(128)S(1)}, f32[128]{0:T(128)}, u32[]{:S(2)}) copy-start(f32[128]{0:T(128)} %constant.247) | copy-start | bytes 1540
  2.2 24.0 %copy-start.13 = (f32[128]{0:T(128)S(1)}, f32[128]{0:T(128)}, u32[]{:S(2)}) copy-start(f32[128]{0:T(128)} %constant.246) | copy-start | bytes 1540
  2.2 24.0 %copy-start.14 = (f32[128]{0:T(128)S(1)}, f32[128]{0:T(128)}, u32[]{:S(2)}) copy-start(f32[128]{0:T(128)} %constant.245) | copy-start | bytes 1540
  2.2 24.0 %copy-start.15 = (pred[128]{0:T(512)(128)(4,1)S(1)}, pred[128]{0:T(512)(128)(4,1)}, u32[]{:S(2)}) copy-start(pred[128]{0:T(512)(128)(4,1)} %constant.243) | copy-start | bytes 388
  2.2 24.0 %copy-start.16 = (pred[128]{0:T(512)(128)(4,1)S(1)}, pred[128]{0:T(512)(128)(4,1)}, u32[]{:S(2)}) copy-start(pred[128]{0:T(512)(128)(4,1)} %constant.241) | copy-start | bytes 388
  2.2 24.0 %copy-start.17 = (pred[128]{0:T(512)(128)(4,1)S(1)}, pred[128]{0:T(512)(128)(4,1)}, u32[]{:S(2)}) copy-start(pred[128]{0:T(512)(128)(4,1)} %constant.239) | copy-start | bytes 388
  2.2 24.0 %copy-start.18 = (pred[128]{0:T(512)(128)(4,1)S(1)}, pred[128]{0:T(512)(128)(4,1)}, u32[]{:S(2)}) copy-start(pred[128]{0:T(512)(128)(4,1)} %constant.237) | copy-start | bytes 388
  2.2 24.0 %copy-start.19 = (pred[128]{0:T(512)(128)(4,1)S(1)}, pred[128]{0:T(512)(128)(4,1)}, u32[]{:S(2)}) copy-start(pred[128]{0:T(512)(128)(4,1)} %constant.235) | copy-start | bytes 388
  2.2 24.0 %copy-start.20 = (pred[128]{0:T(512)(128)(4,1)S(1)}, pred[128]{0:T(512)(128)(4,1)}, u32[]{:S(2)}) copy-start(pred[128]{0:T(512)(128)(4,1)} %constant.233) | copy-start | bytes 388
  2.3 24.0 %copy-start.21 = (pred[128]{0:T(512)(128)(4,1)S(1)}, pred[128]{0:T(512)(128)(4,1)}, u32[]{:S(2)}) copy-start(pred[128]{0:T(512)(128)(4,1)} %constant.231) | copy-start | bytes 388
  2.3 24.0 %copy-start.22 = (pred[128]{0:T(512)(128)(4,1)S(1)}, pred[128]{0:T(512)(128)(4,1)}, u32[]{:S(2)}) copy-start(pred[128]{0:T(512)(128)(4,1)} %constant.229) | copy-start | bytes 388
  2.3 24.0 %copy-start.23 = (pred[128]{0:T(512)(128)(4,1)S(1)}, pred[128]{0:T(512)(128)(4,1)}, u32[]{:S(2)}) copy-start(pred[128]{0:T(512)(128)(4,1)} %constant.227) | copy-start | bytes 388
  2.3 24.0 %copy-start.24 = (pred[128]{0:T(512)(128)(4,1)S(1)}, pred[128]{0:T(512)(128)(4,1)}, u32[]{:S(2)}) copy-start(pred[128]{0:T(512)(128)(4,1)} %constant.225) | copy-start | bytes 388
  2.3 24.0 %copy-start.25 = (f32[128]{0:T(128)S(1)}, f32[128]{0:T(128)}, u32[]{:S(2)}) copy-start(f32[128]{0:T(128)} %constant.223) | copy-start | bytes 1540
  2.3 24.0 %copy-start.26 = (pred[128]{0:T(512)(128)(4,1)S(1)}, pred[128]{0:T(512)(128)(4,1)}, u32[]{:S(2)}) copy-start(pred[128]{0:T(512)(128)(4,1)} %constant.222) | copy-start | bytes 388
  2.3 24.0 %copy-start.27 = (f32[128]{0:T(128)S(1)}, f32[128]{0:T(128)}, u32[]{:S(2)}) copy-start(f32[128]{0:T(128)} %constant.220) | copy-start | bytes 1540
  2.3 24.0 %copy-start.28 = (pred[128]{0:T(512)(128)(4,1)S(1)}, pred[128]{0:T(512)(128)(4,1)}, u32[]{:S(2)}) copy-start(pred[128]{0:T(512)(128)(4,1)} %constant.219) | copy-start | bytes 388
  2.5 57.1 %copy-start.2 = (f32[128,256]{1,0:T(8,128)S(1)}, f32[128,256]{1,0:T(8,128)}, u32[]{:S(2)}) copy-start(f32[128,256]{1,0:T(8,128)} %constant.186.clone.waves_ref) | copy-start | bytes 393220
  2.5 57.1 %copy-start.3 = (s32[128,128]{1,0:T(8,128)S(1)}, s32[128,128]{1,0:T(8,128)}, u32[]{:S(2)}) copy-start(s32[128,128]{1,0:T(8,128)} %constant.187.clone.gap_ref) | copy-start | bytes 196612
  13.0 5.0 %collective-permute-start = (f32[256,512]{1,0:T(8,128)}, f32[256,512]{1,0:T(8,128)S(1)}, u32[]{:S(2)}, u32[]{:S(2)}) collective-permute-start(f32[256,512]{1,0:T(8,128)} %get-tuple-element.15), channel_id=1, source_target_pairs={{0,1},{1,0},{2,3},{3,2},{4,5},{5,4},{6,7},{7,6},{8,9},{9,8},{10,11... | collective-permute-start | bytes 1572872 | tf_op jit(solution)/shard_map/ppermute | solution.py:379
  20.3 42.0 %copy-start.40 = (f32[2,120]{1,0:T(2,128)S(1)}, f32[2,120]{1,0:T(2,128)}, u32[]{:S(2)}) copy-start(f32[2,120]{1,0:T(2,128)} %constant.188.clone) | copy-start | bytes 2884
  20.8 15.8 %all-to-all-start = ((f32[16,64,128]{2,1,0:T(8,128)}), f32[16,64,128]{2,1,0:T(8,128)S(1)}, u32[]{:S(2)}, u32[]{:S(2)}) async-start(f32[16,64,128]{2,1,0:T(8,128)} %pack.1), calls=%async_computation | async-start | bytes 1048576 | tf_op jit(solution)/shard_map/all_to_all | solution.py:387
  37.4 18.2 %all-to-all-start.1 = ((f32[8,72,128]{2,1,0:T(8,128)}), f32[8,72,128]{2,1,0:T(8,128)S(1)}, u32[]{:S(2)}, u32[]{:S(2)}) async-start(f32[8,72,128]{2,1,0:T(8,128)} %plane.1), calls=%async_computation.1 | async-start | bytes 589824 | tf_op jit(solution)/shard_map/all_to_all | solution.py:390
  55.6 6.7 %collective-permute-start.1 = (f32[64,128]{1,0:T(8,128)S(1)}, f32[64,128]{1,0:T(8,128)S(1)}, u32[]{:S(2)}, u32[]{:S(2)}) collective-permute-start(f32[64,128]{1,0:T(8,128)S(1)} %slice_reduce_fusion.own_ref), channel_id=1, source_target_pairs={{0,1},{1,0},{2,3},{3,2},{4,5},{5,4},{6,7},{7,6},{8,9},{9,8},{10,11... | collective-permute-start | bytes 98312 | tf_op jit(solution)/shard_map/ppermute | solution.py:392
  64.1 12.5 %all-to-all-start.2 = ((f32[16,40,128]{2,1,0:T(8,128)}), f32[16,40,128]{2,1,0:T(8,128)S(1)}, u32[]{:S(2)}, u32[]{:S(2)}) async-start(f32[16,40,128]{2,1,0:T(8,128)} %far.1), calls=%async_computation.2 | async-start | bytes 655360 | tf_op jit(solution)/shard_map/all_to_all | solution.py:441
  (14 other events, 304.1 us)

commit v3 on v2

--- a/solution.py
+++ b/solution.py
@@ -50,21 +50,32 @@
     return degree, order, size, rise, fall, link, unit
 
 
-def radial(cos_theta, sine_theta):
-    degree, order, size, rise, fall, link, _ = index_tables()
-    row = lambda v: jnp.asarray(np.asarray(v, np.float32)[None, :])
-    current = jnp.full((cos_theta.shape[0], LANES), 1.0 / math.sqrt(4.0 * math.pi), F32)
+def constants():
+    degree, order, size, rise, fall, link, unit = index_tables()
+    rows = [order, degree, size, link, unit.real, unit.imag, 0 * size, 0 * size]
+    table = np.zeros((32, LANES), np.float32)
+    table[:8] = np.stack(rows)
+    table[8 : 8 + ORDER] = rise[1:]
+    table[20 : 20 + ORDER] = fall[1:]
+    return table
+
+
+def radial(const_ref, theta):
+    order, degree, size, link = (const_ref[r : r + 1] for r in range(4))
+    cos_theta, sine_theta = jnp.cos(theta), jnp.sin(theta)
+    current = jnp.full(theta.shape, 1.0 / math.sqrt(4.0 * math.pi), F32)
     for t in range(1, ORDER + 1):
         factor = -math.sqrt((2.0 * t + 1.0) / (2.0 * t))
-        current = jnp.where(row(size) >= t, factor * sine_theta * current, current)
+        current = jnp.where(size >= t, factor * sine_theta * current, current)
     previous = jnp.zeros_like(current)
     for t in range(1, ORDER + 1):
-        following = row(rise[t]) * (cos_theta * current - row(fall[t]) * previous)
-        on = row(rise[t]) > 0
-        previous, current = jnp.where(on, current, previous), jnp.where(on, following, current)
-    pi_term = row(order) * current / sine_theta
-    tau_term = (row(degree) * cos_theta * current - row(link) * previous) / sine_theta
-    return jnp.stack([tau_term + pi_term, tau_term - pi_term])
+        rise, fall = const_ref[7 + t : 8 + t], const_ref[19 + t : 20 + t]
+        following = rise * (cos_theta * current - fall * previous)
+        previous = jnp.where(rise > 0, current, previous)
+        current = jnp.where(rise > 0, following, current)
+    pi_term = order * current / sine_theta
+    tau_term = (degree * cos_theta * current - link * previous) / sine_theta
+    return tau_term + pi_term, tau_term - pi_term, sine_theta
 
 
 def halves(value):
@@ -85,14 +96,13 @@
     return out
 
 
-def call(body, outs, ins, name, flops=1, limit=16, **kw):
+def call(body, outs, ins, flops=1, limit=16, **kw):
     size = sum(math.prod(a.shape) * a.dtype.itemsize for a in list(outs) + list(ins))
     return pl.pallas_call(
         body,
         out_shape=[jax.ShapeDtypeStruct(o.shape, o.dtype) for o in outs],
         compiler_params=pltpu.CompilerParams(vmem_limit_bytes=limit * 1024 * 1024),
         cost_estimate=pl.CostEstimate(flops=flops, bytes_accessed=size, transcendentals=0),
-        name=name,
         **kw,
     )(*ins)
 
@@ -102,7 +112,7 @@
 
 
 def move_kernel(
-    unroll, scalar_ref, coef_hbm, table_hbm, weight_ref, mine_ref, theirs_ref,
+    unroll, core_ref, cell_ref, coef_hbm, table_hbm, weight_ref, mine_ref, theirs_ref,
     coef, table, total, absorbed, right, sems,
 ):
     spheres = coef.shape[0]
@@ -113,9 +123,8 @@
 
     def table_copy(j, stage):
         axis = 2 - stage
-        cell = scalar_ref[1 + 3 * j + axis]
         return pltpu.make_async_copy(
-            table_hbm.at[axis, cell], table.at[stage, j], sems.at[stage, j]
+            table_hbm.at[axis, cell_ref[axis, j]], table.at[stage, j], sems.at[stage, j]
         )
 
     def fetches(group):
@@ -166,19 +175,23 @@
         if group + 1 < groups:
             first, second = ahead
     total[0, COEFS : COEFS + 1] = jnp.sum(absorbed[...], axis=0, keepdims=True)
-    core = scalar_ref[0]
-    mine_ref[...] = total[core]
-    theirs_ref[...] = total[1 - core]
+    core = core_ref[0]
+    for part, out_ref in ((core, mine_ref), (1 - core, theirs_ref)):
+        for tile in range(4):
+            lanes = slice(tile * LANES, (tile + 1) * LANES)
+            blocks = [total[part, g * 64 : (g + 1) * 64, lanes] for g in range(4)]
+            for x, block in enumerate(swap_chunks(blocks)):
+                out_ref[4 * tile + x] = block
 
 
 def moved_sum(coefficients, positions, shift_tables, absorb_weight, core, unroll=2):
     spheres = coefficients.shape[0]
-    scalars = jnp.concatenate([core.reshape(1), positions.reshape(-1)])
+    smem = pl.BlockSpec(memory_space=pltpu.SMEM)
     hbm = pl.BlockSpec(memory_space=pltpu.HBM)
     vmem = pl.BlockSpec(memory_space=pltpu.VMEM)
     return pl.pallas_call(
         functools.partial(move_kernel, unroll),
-        in_specs=[pl.BlockSpec(memory_space=pltpu.SMEM), hbm, hbm, vmem],
+        in_specs=[smem, smem, hbm, hbm, vmem],
         out_specs=[vmem, vmem],
         scratch_shapes=[
             pltpu.VMEM((spheres, COEFS, 2 * FIELDS), BF16),
@@ -188,27 +201,13 @@
             pltpu.VMEM((unroll, 2 * ROWS, FIELDS), BF16),
             pltpu.SemaphoreType.DMA((4, spheres)),
         ],
-        out_shape=[struct((ROWS, FIELDS))] * 2,
-        compiler_params=pltpu.CompilerParams(vmem_limit_bytes=62 * 1024 * 1024),
+        out_shape=[struct((16, 64, LANES))] * 2,
+        compiler_params=pltpu.CompilerParams(vmem_limit_bytes=52 * 1024 * 1024),
         cost_estimate=pl.CostEstimate(
             flops=6_000_000_000, bytes_accessed=10_000_000, transcendentals=0
         ),
         name="move",
-    )(scalars, coefficients, shift_tables, absorb_weight)
-
-
-def pack_kernel(mine_ref, other_ref, detector_ref, out_ref):
-    detector = detector_ref[...]
-    detector = jnp.concatenate([detector[:, :CHUNK], detector[:, CHUNK:]], axis=0)
-    for tile in range(4):
-        lanes = slice(tile * LANES, (tile + 1) * LANES)
-        blocks = [
-            mine_ref[g * 64 : (g + 1) * 64, lanes] + other_ref[g * 64 : (g + 1) * 64, lanes]
-            for g in range(4)
-        ]
-        for x, block in enumerate(swap_chunks(blocks)):
-            out_ref[4 * tile + x] = block
-            out_ref[4 * tile + x, 56:, 96:] = detector
+    )(core, positions.T, coefficients, shift_tables, absorb_weight)
 
 
 def plane_kernel(got_ref, out_ref):
@@ -226,14 +225,51 @@
         out_ref[k, 64:] = detectors
 
 
-def basis_kernel(radial_ref, cos_ref, sin_ref, high_ref, low_ref):
-    for sign in range(2):
-        for trig, ref in enumerate((cos_ref, sin_ref)):
-            block = radial_ref[sign][None, :, None, :] * ref[...].reshape(4, 1, 8, LANES)
+def tables_kernel(
+    place_ref, const_ref, high_ref, low_ref, whole_ref, scaled_ref, gap_ref, waves_ref, phase_ref
+):
+    z, core = place_ref[0], place_ref[1]
+    row = lambda shape: lax.broadcasted_iota(jnp.int32, shape, 0)
+    step = math.pi / POLAR
+
+    near = row((16, LANES))
+    near = ((near // 4) * 8 + z) * 4 + near % 4
+    plus, minus, _ = radial(const_ref, (near.astype(F32) + 0.5) * step)
+    azim = row((32, LANES))
+    azim = ((azim // 8) * 2 + core) * 8 + azim % 8
+    turn = (azim * const_ref[0:1].astype(jnp.int32)) & (AZIM - 1)
+    angle = turn.astype(F32) * (2.0 * math.pi / AZIM)
+    for sign, table in enumerate((plus, minus)):
+        for trig, wave in enumerate((jnp.cos(angle), jnp.sin(angle))):
+            block = table[None, :, None, :] * wave.reshape(4, 1, 8, LANES)
             high, low = halves(block.reshape(2 * ROWS, LANES))
             lanes = slice((2 * sign + trig) * LANES, (2 * sign + trig + 1) * LANES)
             high_ref[:, lanes] = high
             low_ref[:, lanes] = low
+
+    plus, minus, sine_theta = radial(
+        const_ref, (row((POLAR, LANES)).astype(F32) + 0.5) * step
+    )
+    weight = sine_theta * (2.0 * math.pi * math.pi / (POLAR * AZIM))
+    for sign, table in enumerate((plus, minus)):
+        whole_ref[sign] = table
+        scaled_ref[sign] = table * weight
+
+    across = lambda r: jnp.broadcast_to(const_ref[r : r + 1], (LANES, LANES))
+    used = across(1) > 0
+    order = across(0)
+    gap = jnp.where(used, order, 200.0) - jnp.where(used, order, 100.0).T
+    gap_ref[...] = gap
+    phase_ref[0] = across(4).T
+    phase_ref[1] = across(5).T
+
+    shape = (LANES, LANES)
+    lane = lax.broadcasted_iota(jnp.int32, shape, 1)
+    for half in range(2):
+        azim = row(shape) % CHUNK + half * CHUNK
+        turn = (azim * (lane % 64) - jnp.where(lane < 64, 0, AZIM // 4)) & (AZIM - 1)
+        wave = jnp.cos(turn.astype(F32) * (2.0 * math.pi / AZIM))
+        waves_ref[:, half * LANES : (half + 1) * LANES] = wave
 
 
 def power_kernel(radial_ref, scaled_ref, line_ref, waves_ref, gap_ref, out_ref):
@@ -288,7 +324,7 @@
     imag = spread_rows(jnp.where(core == 0, other, own))
     group = lax.broadcasted_iota(jnp.int32, (HALF, LANES), 1) // CHUNK
     spare = jnp.zeros((8, LANES), F32)
-    phase_real, phase_imag = phase_ref[0], phase_ref[1]
+    phase_real, phase_imag = phase_ref[0, :HALF], phase_ref[1, :HALF]
     real_1, real_2 = real[:HALF], real[HALF:COEFS]
     imag_1, imag_2 = imag[:HALF], imag[HALF:COEFS]
     rows = []
@@ -374,67 +410,49 @@
     vmem = pl.BlockSpec(memory_space=pltpu.VMEM)
 
     mine, theirs = moved_sum(
-        coefficients, positions, shift_tables, absorb_weight, core.astype(jnp.int32)
+        coefficients, positions, shift_tables, absorb_weight, core.reshape(1)
     )
     other = lax.ppermute(theirs, PAIR, [(0, 1), (1, 0)])
-    (packed,) = call(pack_kernel, [struct((16, 64, LANES))], [mine, other, detector], "pack")
-    packed, incident, z, y, core, polar = lax.optimization_barrier(
-        (packed, incident, z, y, core, jnp.arange(POLAR))
-    )
-    (spread,) = call(
-        plane_kernel,
-        [struct((8, 72, LANES))],
-        [lax.all_to_all(packed, PLANE, 0, 0, tiled=True)],
-        "plane",
-    )
+    share = jnp.concatenate([detector[:, :CHUNK], detector[:, CHUNK:]], axis=0)
+    packed = mine + other + jnp.pad(share, ((56, 0), (96, 0)))[None]
+    packed, incident, x, z, y, core = lax.optimization_barrier(
+        (packed, incident, x, z, y, core)
+    )
+    high, low, whole, scaled, gap, waves, phase = call(
+        tables_kernel,
+        [
+            struct((2 * ROWS, 2 * ROWS), BF16), struct((2 * ROWS, 2 * ROWS), BF16),
+            struct((2, POLAR, LANES)), struct((2, POLAR, LANES)), struct((LANES, LANES)),
+            struct((LANES, 2 * LANES)), struct((2, LANES, LANES)),
+        ],
+        [jnp.stack([z, core]), jnp.asarray(constants())],
+        flops=100_000_000,
+        in_specs=[smem, vmem],
+    )
+    first = (4 * y + x) * CHUNK
+    tables = (
+        whole, scaled, waves, gap, high, low, phase,
+        lax.dynamic_slice_in_dim(incident, first, CHUNK, 1),
+        lax.dynamic_slice_in_dim(incident, FIELDS + first, CHUNK, 1),
+        core.astype(jnp.int32).reshape(1), (4 * y + 2 * core).astype(jnp.int32).reshape(1),
+    )
+    got = lax.all_to_all(packed, PLANE, 0, 0, tiled=True)
+    got, tables = lax.optimization_barrier((got, tables))
+    whole, scaled, waves, gap, high, low, phase, inc_real, inc_imag, core, place = tables
+    (spread,) = call(plane_kernel, [struct((8, 72, LANES))], [got])
     line = lax.all_to_all(spread, LINE, 0, 0, tiled=True)
     own = line[:, :64].sum(axis=0)
     partner = lax.ppermute(own, PAIR, [(0, 1), (1, 0)])
-
-    degree, order, size, rise, fall, link, unit = index_tables()
-    theta = (polar.astype(F32) + 0.5) * (math.pi / POLAR)
-    cos_theta, sine_theta = jnp.cos(theta)[:, None], jnp.sin(theta)[:, None]
-    whole = radial(cos_theta, sine_theta)
-    solid_angle = 2.0 * math.pi * math.pi / (POLAR * AZIM)
-    scaled = whole * (sine_theta * solid_angle)
-    near_polar = ((jnp.arange(4) * 8 + z)[:, None] * 4 + jnp.arange(4)[None, :]).reshape(-1)
-    near_theta = (near_polar.astype(F32) + 0.5) * (math.pi / POLAR)
-    near = radial(jnp.cos(near_theta)[:, None], jnp.sin(near_theta)[:, None])
-    near_azim = ((jnp.arange(4) * 2 + core)[:, None] * 8 + jnp.arange(8)[None, :]).reshape(-1)
-    azimuth = near_azim.astype(F32) * (2.0 * math.pi / AZIM)
-    angle = azimuth[:, None] * jnp.asarray(np.asarray(order, np.float32))[None, :]
-    high, low = call(
-        basis_kernel,
-        [struct((2 * ROWS, 2 * ROWS), BF16)] * 2,
-        [near, jnp.cos(angle), jnp.sin(angle)],
-        "basis",
-        flops=10_000_000,
-    )
-    turns = np.arange(AZIM)[:, None] * np.arange(2 * ORDER + 1)[None, :] % AZIM
-    waves = np.zeros((AZIM, LANES), np.float32)
-    waves[:, : 2 * ORDER + 1] = np.cos(2.0 * math.pi * turns / AZIM)
-    waves[:, 64 : 64 + 2 * ORDER + 1] = np.sin(2.0 * math.pi * turns / AZIM)
-    waves = np.tile(np.concatenate([waves[:CHUNK], waves[CHUNK:]], axis=1), (4, 1))
-    gap = np.where((degree[:, None] > 0) & (degree[None, :] > 0), order[None, :] - order[:, None], 99)
     (form,) = call(
         power_kernel,
         [struct((2, LANES, 2 * LANES))],
-        [whole, scaled, line, jnp.asarray(waves), jnp.asarray(gap.astype(np.int32))],
-        "power",
+        [whole, scaled, line, waves, gap],
         flops=1_000_000_000,
     )
-    first = (4 * y + x) * CHUNK
-    phase = np.stack([unit.real[:HALF], unit.imag[:HALF]]).astype(np.float32)
-    phase = jnp.asarray(np.broadcast_to(phase[:, :, None], (2, HALF, LANES)))
     (messages,) = call(
         far_kernel,
         [struct((16, 40, LANES))],
-        [
-            core.astype(jnp.int32).reshape(1), own, partner, high, low, form, phase,
-            lax.dynamic_slice_in_dim(incident, first, CHUNK, 1),
-            lax.dynamic_slice_in_dim(incident, FIELDS + first, CHUNK, 1),
-        ],
-        "far",
+        [core, own, partner, high, low, form, phase, inc_real, inc_imag],
         flops=400_000_000,
         in_specs=[smem] + [vmem] * 8,
     )
@@ -442,8 +460,7 @@
     amplitude, stats = call(
         finish_kernel,
         [struct((4, 32, FIELDS)), struct((3, 64))],
-        [(4 * y + 2 * core).astype(jnp.int32).reshape(1), got],
-        "finish",
+        [place, got],
         in_specs=[smem, vmem],
     )
     return (amplitude.reshape(2, 2, 4, 8, FIELDS), stats)

time: 78 us -> 72.8 us (0.933)
  blocking collectives: 0 us -> 30 us
  waiting for transfers between devices: 25 us -> 8.97 us
  starting transfers between devices: 24.2 us -> 12.6 us
  other arithmetic: 5.37 us -> 1.03 us
  Pallas kernels: 18.1 us -> 16.6 us
  local copies, waits for them, and re-layouts: 3.57 us -> 2.54 us
    all_to_all x0 -> x2, blocking collectives: none -> 30 us  [the longest x1 17.7 us: shards(): line = lax.all_to_all(spread, LINE, 0, 0, tiled=True)]
    all_to_all x3 -> x1, waiting for transfers between devices: 23.2 us -> 7.58 us  [shards(): got = lax.all_to_all(packed, PLANE, 0, 0, tiled=True)]
    all_to_all x3 -> x1, starting transfers between devices: 17 us -> 4.73 us  [shards(): got = lax.all_to_all(packed, PLANE, 0, 0, tiled=True)]
    sub x2 -> x0, other arithmetic: 2.14 us -> none  [radial(): return jnp.stack([tau_term + pi_term, tau_term - pi_term])]
    add x2 -> x1, other arithmetic: 2.14 us -> 0.86 us  [shards(): packed = mine + other + jnp.pad(share, ((56, 0), (96, 0)))[None]]
    pallas_call x6 -> x5, Pallas kernels: 7.6 us -> 6.58 us  [call(): pl.pallas_call(body, out_shape=[jax.ShapeDtypeStruct(o.shape, o.dtype) fo...]
    unnamed x83 -> x8, local copies, waits for them, and re-layouts: 2.06 us -> 1.38 us
  transfers between devices with their start and end apart: 5 -> 3, of which waited for: 4 -> 2; matrix products, arithmetic and copies ran while one was open for 7% -> 2% of each run, Pallas kernels for 4% -> 6%
where the time goes in v3:
time: 72.8 us; the launch traced here: 72.4 us
  blocking collectives  30 us (41%)
  Pallas kernels  16.6 us (23%)
  starting transfers between devices  12.6 us (17%)
  waiting for transfers between devices  8.97 us (12%)
  local copies, waits for them, and re-layouts  2.54 us (3%)
  other arithmetic  1.03 us (1%)
    all_to_all x1, blocking collectives, shards(): line = lax.all_to_all(spread, LINE, 0, 0, tiled=True)  17.7 us
    all_to_all x1, blocking collectives, shards(): got = lax.all_to_all(messages, PLANE, 0, 0, tiled=True)  12.3 us
    pallas_call x1, Pallas kernels, moved_sum(): pl.pallas_call(functools.partial(move_kernel, unroll), in_specs=[smem, sm...  10 us
    all_to_all x1, waiting for transfers between devices, shards(): got = lax.all_to_all(packed, PLANE, 0, 0, tiled=True)  7.58 us
    pallas_call x5, Pallas kernels, call(): pl.pallas_call(body, out_shape=[jax.ShapeDtypeStruct(o.shape, o.dtype) fo...  6.58 us
    all_to_all x1, starting transfers between devices, shards(): got = lax.all_to_all(packed, PLANE, 0, 0, tiled=True)  4.73 us
    ppermute x1, starting transfers between devices, shards(): partner = lax.ppermute(own, PAIR, [(0, 1), (1, 0)])  4.25 us
    ppermute x1, starting transfers between devices, shards(): other = lax.ppermute(theirs, PAIR, [(0, 1), (1, 0)])  3.6 us
  transfers between devices with their start and end apart: 3, of which 2 were waited for; matrix products, arithmetic and copies ran while one was open for 2% of the time, Pallas kernels for 6%

profile of v3, /device:TPU:1, one launch (start us, length us, event | category | flops | bytes accessed | tf_op | source)
XLA Modules:
  0.0 72.4 jit_solution(14121566909630822367)
XLA Ops:
  0.6 0.0 copy-start
  0.6 0.7 copy-done
  1.3 0.0 copy-start.1
  1.3 0.7 copy-done.1
  2.0 0.0 copy-start.3
  2.0 0.0 copy-start.2
  2.0 10.0 %move.1 = (f32[16,64,128]{2,1,0:T(8,128)S(1)}, f32[16,64,128]{2,1,0:T(8,128)S(1)}) custom-call(s32[1]{0:T(128)} %bitcast.core_ref, s32[3,8]{1,0:T(4,128)S(1)} %bitcast.6, bf16[8,240,1024]{2,1,0:T(8,128)(2,1)} %coef_hbm.1, bf16[3,8,480,240]{3,2,1,0:T(8,128)(2,1)} %table_hbm.1, f32[8,240]{1,0:T(8,128)S(1)} %copy-done), custom_call_target="tpu_custom_call" | custom-call | flops 6000000000 | bytes 10000000 | tf_op jit(solution)/shard_map/move/pallas_call | solution.py:192
  12.1 3.6 %collective-permute-start = (f32[16,64,128]{2,1,0:T(8,128)S(1)}, f32[16,64,128]{2,1,0:T(8,128)S(1)}, u32[]{:S(2)}, u32[]{:S(2)}) collective-permute-start(f32[16,64,128]{2,1,0:T(8,128)S(1)} %get-tuple-element.32), channel_id=1, source_target_pairs={{0,1},{1,0},{2,3},{3,2},{4,5},{5,4},{6,7},{7,6},{8,9},{9,8},{10,11... | collective-permute-start | bytes 1572872 | tf_op jit(solution)/shard_map/ppermute | solution.py:415
  15.7 0.0 copy-done.3
  15.7 0.1 fusion
  15.7 0.1 select_maximum_fusion
  15.8 1.4 %collective-permute-done = f32[16,64,128]{2,1,0:T(8,128)S(1)} collective-permute-done((f32[16,64,128]{2,1,0:T(8,128)S(1)}, f32[16,64,128]{2,1,0:T(8,128)S(1)}, u32[]{:S(2)}, u32[]{:S(2)}) %collective-permute-start) | collective-permute-done | bytes 524320 | tf_op jit(solution)/shard_map/ppermute | solution.py:415
  17.2 0.9 %add_add_fusion = f32[16,64,128]{2,1,0:T(8,128)} fusion(f32[16,64,128]{2,1,0:T(8,128)S(1)} %get-tuple-element.31, f32[16,64,128]{2,1,0:T(8,128)S(1)} %collective-permute-done, f32[64,128]{1,0:T(8,128)S(1)} %select_maximum_fusion), kind=kLoop, calls=%fused_computation | loop fusion | flops 262144 | bytes 1605632 | tf_op jit(solution)/shard_map/add | solution.py:417
  18.1 4.7 %all-to-all-start = ((f32[16,64,128]{2,1,0:T(8,128)}), f32[16,64,128]{2,1,0:T(8,128)S(1)}, u32[]{:S(2)}, u32[]{:S(2)}) async-start(f32[16,64,128]{2,1,0:T(8,128)} %add_add_fusion), calls=%async_computation | async-start | bytes 1048576 | tf_op jit(solution)/shard_map/all_to_all | solution.py:439
  22.8 0.1 pad_add_fusion.place_ref
  22.9 0.0 copy-done.2
  22.9 1.9 %shard_map.86 = (bf16[512,512]{1,0:T(8,128)(2,1)S(1)}, bf16[512,512]{1,0:T(8,128)(2,1)S(1)}, f32[2,128,128]{2,1,0:T(8,128)S(1)}, f32[2,128,128]{2,1,0:T(8,128)S(...) custom-call(s32[2]{0:T(128)S(1)} %pad_add_fusion.place_ref, f32[32,128]{1,0:T(8,128)S(1)} %copy-done.2), custom_call_target="tpu_custom_call" | custom-call | flops 100000000 | bytes 1654792 | tf_op jit(solution)/shard_map/pallas_call | solution.py:101
  24.8 1.1 %constant_dynamic-slice_fusion = (f32[240,32]{1,0:T(8,128)S(1)}, f32[240,32]{1,0:T(8,128)S(1)}) fusion(f32[240,1024]{1,0:T(8,128)} %param.11, s32[]{:T(128)S(6)} %select_n.7, s32[]{:T(128)S(6)} %select_n.6), kind=kLoop, calls=%fused_computation.6 | loop fusion | bytes 122888 | tf_op jit(solution)/shard_map/dynamic_slice | solution.py:436
  25.9 7.6 %all-to-all-done.got_ref = f32[16,64,128]{2,1,0:T(8,128)S(1)} async-done(((f32[16,64,128]{2,1,0:T(8,128)}), f32[16,64,128]{2,1,0:T(8,128)S(1)}, u32[]{:S(2)}, u32[]{:S(2)}) %all-to-all-start) | async-done | bytes 524320 | tf_op jit(solution)/shard_map/all_to_all | solution.py:439
  33.5 0.1 shard_map.87
  33.6 17.7 %all_to_all.15.line_ref = f32[8,72,128]{2,1,0:T(8,128)S(1)} all-to-all(f32[8,72,128]{2,1,0:T(8,128)S(1)} %shard_map.87), channel_id=1, replica_groups=mesh['sph_0'=4,'sph_1'=8,'ang_0'=4,'ang_1'=2] {'sph_1'}, dimensions={0} | all-to-all | bytes 589824 | tf_op jit(solution)/shard_map/all_to_all | solution.py:443
  51.3 4.2 %collective-permute-start.1 = (f32[64,128]{1,0:T(8,128)S(1)}, f32[64,128]{1,0:T(8,128)S(1)}, u32[]{:S(2)}, u32[]{:S(2)}) collective-permute-start(f32[64,128]{1,0:T(8,128)S(1)} %slice_reduce_fusion.own_ref), channel_id=1, source_target_pairs={{0,1},{1,0},{2,3},{3,2},{4,5},{5,4},{6,7},{7,6},{8,9},{9,8},{10,11... | collective-permute-start | bytes 98312 | tf_op jit(solution)/shard_map/ppermute | solution.py:445
  55.6 2.7 %shard_map.88.form_ref = f32[2,128,256]{2,1,0:T(8,128)S(1)} custom-call(f32[2,128,128]{2,1,0:T(8,128)S(1)} %get-tuple-element.51.radial_ref, f32[2,128,128]{2,1,0:T(8,128)S(1)} %get-tuple-element.52.scaled_ref, f32[8,72,128]{2,1,0:T(8,128)S(1)} %all_to_all.15.line_ref, f32[128,256]{1,0:T(8,128)S(1)} %get-tuple-element.53.waves_ref, ...), custom_call_target="tpu_custom_call" | custom-call | flops 1000000000 | bytes 1015808 | tf_op jit(solution)/shard_map/pallas_call | solution.py:101
  58.2 0.0 collective-permute-done.1.other_ref
  58.2 0.9 %shard_map.89 = f32[16,40,128]{2,1,0:T(8,128)S(1)} custom-call(s32[1]{0:T(128)} %bitcast.3.core_ref, f32[64,128]{1,0:T(8,128)S(1)} %slice_reduce_fusion.own_ref, f32[64,128]{1,0:T(8,128)S(1)} %collective-permute-done.1.other_ref, bf16[512,512]{1,0:T(8,128)(2,1)S(1)} %get-tuple-element.49.high_ref, bf16[512,512]{1,0:T(8,128)(2,1)S(1)} %get-tuple-element.50.low_ref, ...), custom_call_target="tpu_custom_call" | custom-call | flops 400000000 | bytes 1896452 | tf_op jit(solution)/shard_map/pallas_call | solution.py:101
  59.2 12.3 %all_to_all.16.got_ref = f32[16,40,128]{2,1,0:T(8,128)S(1)} all-to-all(f32[16,40,128]{2,1,0:T(8,128)S(1)} %shard_map.89), channel_id=1, replica_groups=mesh['sph_0'=4,'sph_1'=8,'ang_0'=4,'ang_1'=2] {'ang_0','sph_0'}, dimensions={0} | all-to-all | bytes 655360 | tf_op jit(solution)/shard_map/all_to_all | solution.py:459
  71.4 1.0 %shard_map.90 = (f32[4,32,512]{2,1,0:T(8,128)}, f32[3,64]{1,0:T(4,128)}) custom-call(s32[1]{0:T(128)} %bitcast.4.place_ref, f32[16,40,128]{2,1,0:T(8,128)S(1)} %all_to_all.16.got_ref), custom_call_target="tpu_custom_call" | custom-call | flops 1 | bytes 590596 | tf_op jit(solution)/shard_map/pallas_call | solution.py:101
  (1 shorter events, 0.0 us)
Async XLA Ops:
  0.6 0.7 copy-start
  1.3 0.7 copy-start.1
  2.0 13.6 %copy-start.3 = (f32[4,64]{1,0:T(4,128)S(1)}, f32[4,64]{1,0:T(4,128)}, u32[]{:S(2)}) copy-start(f32[4,64]{1,0:T(4,128)} %param.12) | copy-start | bytes 3076
  2.0 20.9 %copy-start.2 = (f32[32,128]{1,0:T(8,128)S(1)}, f32[32,128]{1,0:T(8,128)}, u32[]{:S(2)}) copy-start(f32[32,128]{1,0:T(8,128)} %constant.35.clone.const_ref) | copy-start | bytes 49156
  12.1 5.1 %collective-permute-start = (f32[16,64,128]{2,1,0:T(8,128)S(1)}, f32[16,64,128]{2,1,0:T(8,128)S(1)}, u32[]{:S(2)}, u32[]{:S(2)}) collective-permute-start(f32[16,64,128]{2,1,0:T(8,128)S(1)} %get-tuple-element.32), channel_id=1, source_target_pairs={{0,1},{1,0},{2,3},{3,2},{4,5},{5,4},{6,7},{7,6},{8,9},{9,8},{10,11... | collective-permute-start | bytes 1572872 | tf_op jit(solution)/shard_map/ppermute | solution.py:415
  18.1 15.5 %all-to-all-start = ((f32[16,64,128]{2,1,0:T(8,128)}), f32[16,64,128]{2,1,0:T(8,128)S(1)}, u32[]{:S(2)}, u32[]{:S(2)}) async-start(f32[16,64,128]{2,1,0:T(8,128)} %add_add_fusion), calls=%async_computation | async-start | bytes 1048576 | tf_op jit(solution)/shard_map/all_to_all | solution.py:439
  51.3 6.9 %collective-permute-start.1 = (f32[64,128]{1,0:T(8,128)S(1)}, f32[64,128]{1,0:T(8,128)S(1)}, u32[]{:S(2)}, u32[]{:S(2)}) collective-permute-start(f32[64,128]{1,0:T(8,128)S(1)} %slice_reduce_fusion.own_ref), channel_id=1, source_target_pairs={{0,1},{1,0},{2,3},{3,2},{4,5},{5,4},{6,7},{7,6},{8,9},{9,8},{10,11... | collective-permute-start | bytes 98312 | tf_op jit(solution)/shard_map/ppermute | solution.py:445

commit v4 on v3

--- a/solution.py
+++ b/solution.py
@@ -111,9 +111,25 @@
     return jax.ShapeDtypeStruct(shape, dtype)
 
 
+def pack(total, part, out_ref):
+    for tile in range(4):
+        lanes = slice(tile * LANES, (tile + 1) * LANES)
+        blocks = [total[part, g * 64 : (g + 1) * 64, lanes] for g in range(4)]
+        for x, block in enumerate(swap_chunks(blocks)):
+            out_ref[4 * tile + x] = block
+
+
+def pack_kernel(core_ref, total_ref, detector_ref, out_ref):
+    pack(total_ref, core_ref[0], out_ref)
+    detector = detector_ref[...]
+    detector = jnp.concatenate([detector[:, :CHUNK], detector[:, CHUNK:]], axis=0)
+    for k in range(16):
+        out_ref[k, 56:, 96:] = detector
+
+
 def move_kernel(
-    unroll, core_ref, cell_ref, coef_hbm, table_hbm, weight_ref, mine_ref, theirs_ref,
-    coef, table, total, absorbed, right, sems,
+    unroll, core_ref, cell_ref, coef_hbm, table_hbm, weight_ref, total, theirs_ref,
+    coef, table, absorbed, right, sems,
 ):
     spheres = coef.shape[0]
     groups = spheres // unroll
@@ -175,13 +191,7 @@
         if group + 1 < groups:
             first, second = ahead
     total[0, COEFS : COEFS + 1] = jnp.sum(absorbed[...], axis=0, keepdims=True)
-    core = core_ref[0]
-    for part, out_ref in ((core, mine_ref), (1 - core, theirs_ref)):
-        for tile in range(4):
-            lanes = slice(tile * LANES, (tile + 1) * LANES)
-            blocks = [total[part, g * 64 : (g + 1) * 64, lanes] for g in range(4)]
-            for x, block in enumerate(swap_chunks(blocks)):
-                out_ref[4 * tile + x] = block
+    pack(total, 1 - core_ref[0], theirs_ref)
 
 
 def moved_sum(coefficients, positions, shift_tables, absorb_weight, core, unroll=2):
@@ -196,12 +206,11 @@
         scratch_shapes=[
             pltpu.VMEM((spheres, COEFS, 2 * FIELDS), BF16),
             pltpu.VMEM((3, spheres, 2 * COEFS, COEFS), BF16),
-            pltpu.VMEM((2, ROWS, FIELDS), F32),
             pltpu.VMEM((8, FIELDS), F32),
             pltpu.VMEM((unroll, 2 * ROWS, FIELDS), BF16),
             pltpu.SemaphoreType.DMA((4, spheres)),
         ],
-        out_shape=[struct((16, 64, LANES))] * 2,
+        out_shape=[struct((2, ROWS, FIELDS)), struct((16, 64, LANES))],
         compiler_params=pltpu.CompilerParams(vmem_limit_bytes=52 * 1024 * 1024),
         cost_estimate=pl.CostEstimate(
             flops=6_000_000_000, bytes_accessed=10_000_000, transcendentals=0
@@ -274,8 +283,6 @@
 
 def power_kernel(radial_ref, scaled_ref, line_ref, waves_ref, gap_ref, out_ref):
     gap = gap_ref[...]
-    far = jnp.abs(gap)
-    far = jnp.concatenate([far, far], axis=1)
     detectors = line_ref[:, 64:].reshape(64, LANES)
     group = lax.broadcasted_iota(jnp.int32, detectors.shape, 1) // CHUNK
     detectors = jnp.concatenate([jnp.where(group == x, detectors, 0.0) for x in range(4)], axis=0)
@@ -284,22 +291,30 @@
     )
     spectrum = spectrum[:, :LANES] + pltpu.roll(spectrum[:, LANES:], 2 * LANES - 4, 0)
     spectrum = jnp.concatenate([spectrum[8 * k : 8 * k + 4] for k in range(32)], axis=0)
+    spectrum = spectrum.T
+    far = jnp.abs(gap[:HALF])
+    far = jnp.concatenate([far, far], axis=0)
     for sign in range(2):
-        table = scaled_ref[sign]
-        left_high, left_low = halves(radial_ref[sign].T)
-        left = jnp.concatenate([left_high, left_high], axis=1)
-        total = jnp.zeros((LANES, 2 * LANES), F32)
-        for d in range(2 * ORDER + 1):
-            right = jnp.concatenate(
-                [table * spectrum[:, d : d + 1], table * spectrum[:, 64 + d : 65 + d]], axis=1
+        table = scaled_ref[sign].T[:HALF]
+        high, low = halves(radial_ref[sign])
+        fixed = jnp.concatenate([high, low], axis=1)
+        fixed = jnp.concatenate([fixed, fixed], axis=0)
+        total = jnp.zeros((COEFS, LANES), F32)
+        for start in range(0, 2 * ORDER + 1, 7):
+            rows = []
+            for d in range(start, start + 7):
+                rows += [table * spectrum[d : d + 1], table * spectrum[64 + d : 65 + d]]
+            high, low = halves(jnp.concatenate(rows, axis=0))
+            product = jnp.dot(
+                jnp.concatenate([high, low], axis=1), fixed, preferred_element_type=F32
             )
-            high, low = halves(right)
-            product = jnp.dot(
-                left, jnp.concatenate([high, low], axis=0), preferred_element_type=F32
-            ) + jnp.dot(left_low, high, preferred_element_type=F32)
-            total = jnp.where(far == d, product, total)
-        out_ref[sign, :, :LANES] = total[:, :LANES]
-        out_ref[sign, :, LANES:] = jnp.where(gap < 0, -total[:, LANES:], total[:, LANES:])
+            product = product[:, :LANES] + product[:, LANES:]
+            for k in range(7):
+                part = product[k * COEFS : (k + 1) * COEFS]
+                total = jnp.where(far == start + k, part, total)
+        out_ref[sign, 0, :HALF] = total[:HALF]
+        out_ref[sign, 1, :HALF] = jnp.where(gap[:HALF] < 0, -total[HALF:], total[HALF:])
+        out_ref[sign, :, HALF:] = jnp.zeros((2, 8, LANES), F32)
 
 
 def spread_rows(packed):
@@ -348,7 +363,7 @@
         dot = functools.partial(
             jnp.dot, preferred_element_type=F32, precision=lax.Precision.HIGHEST
         )
-        even, odd = form_ref[sign, :, :LANES], form_ref[sign, :, LANES:]
+        even, odd = form_ref[sign, 0], form_ref[sign, 1]
         collected += 0.5 * jnp.sum(
             pair * dot(even, pair)
             + pair_imag * (dot(even, pair_imag) + 2.0 * dot(odd, pair)),
@@ -409,12 +424,18 @@
     smem = pl.BlockSpec(memory_space=pltpu.SMEM)
     vmem = pl.BlockSpec(memory_space=pltpu.VMEM)
 
-    mine, theirs = moved_sum(
+    total, theirs = moved_sum(
         coefficients, positions, shift_tables, absorb_weight, core.reshape(1)
     )
     other = lax.ppermute(theirs, PAIR, [(0, 1), (1, 0)])
-    share = jnp.concatenate([detector[:, :CHUNK], detector[:, CHUNK:]], axis=0)
-    packed = mine + other + jnp.pad(share, ((56, 0), (96, 0)))[None]
+    (mine,) = call(
+        pack_kernel,
+        [struct((16, 64, LANES))],
+        [core.reshape(1), total, detector],
+        flops=10_000_000,
+        in_specs=[smem, vmem, vmem],
+    )
+    packed = mine + other
     packed, incident, x, z, y, core = lax.optimization_barrier(
         (packed, incident, x, z, y, core)
     )
@@ -445,7 +466,7 @@
     partner = lax.ppermute(own, PAIR, [(0, 1), (1, 0)])
     (form,) = call(
         power_kernel,
-        [struct((2, LANES, 2 * LANES))],
+        [struct((2, 2, LANES, LANES))],
         [whole, scaled, line, waves, gap],
         flops=1_000_000_000,
     )

time: 72.8 us -> 72 us (0.989)
    pallas_call x5 -> x6, Pallas kernels: 6.58 us -> 6.67 us  [call(): pl.pallas_call(body, out_shape=[jax.ShapeDtypeStruct(o.shape, o.dtype) fo...]
  transfers between devices with their start and end apart: 3 -> 3, of which waited for: 2 -> 2; matrix products, arithmetic and copies ran while one was open for 2% -> 2% of each run, Pallas kernels for 6% -> 7%
where the time goes in v4:
time: 72 us; the launch traced here: 71.6 us
  blocking collectives  30 us (42%)
  Pallas kernels  16.3 us (23%)
  starting transfers between devices  12.6 us (18%)
  waiting for transfers between devices  8.63 us (12%)
  local copies, waits for them, and re-layouts  2.47 us (3%)
  other arithmetic  0.96 us (1%)
  between operations  0.73 us (1%)
    all_to_all x1, blocking collectives, shards(): line = lax.all_to_all(spread, LINE, 0, 0, tiled=True)  17.7 us
    all_to_all x1, blocking collectives, shards(): got = lax.all_to_all(messages, PLANE, 0, 0, tiled=True)  12.3 us
    pallas_call x1, Pallas kernels, moved_sum(): pl.pallas_call(functools.partial(move_kernel, unroll), in_specs=[smem, sm...  9.63 us
    all_to_all x1, waiting for transfers between devices, shards(): got = lax.all_to_all(packed, PLANE, 0, 0, tiled=True)  7.58 us
    pallas_call x6, Pallas kernels, call(): pl.pallas_call(body, out_shape=[jax.ShapeDtypeStruct(o.shape, o.dtype) fo...  6.67 us
    all_to_all x1, starting transfers between devices, shards(): got = lax.all_to_all(packed, PLANE, 0, 0, tiled=True)  4.73 us
    ppermute x1, starting transfers between devices, shards(): partner = lax.ppermute(own, PAIR, [(0, 1), (1, 0)])  4.25 us
    ppermute x1, starting transfers between devices, shards(): other = lax.ppermute(theirs, PAIR, [(0, 1), (1, 0)])  3.6 us
  transfers between devices with their start and end apart: 3, of which 2 were waited for; matrix products, arithmetic and copies ran while one was open for 2% of the time, Pallas kernels for 7%

profile of v4, /device:TPU:1, one launch (start us, length us, event | category | flops | bytes accessed | tf_op | source)
XLA Modules:
  0.0 71.6 jit_solution(14809274862713682989)
XLA Ops:
  0.6 0.0 copy-start.1
  0.6 0.7 copy-done.1
  1.3 0.0 copy-start.2
  1.3 0.7 copy-done.2
  2.0 0.0 copy-start
  2.0 0.0 copy-start.3
  2.0 9.6 %move.1 = (f32[2,256,512]{2,1,0:T(8,128)S(1)}, f32[16,64,128]{2,1,0:T(8,128)S(1)}) custom-call(s32[1]{0:T(128)} %bitcast.core_ref, s32[3,8]{1,0:T(4,128)S(1)} %bitcast.6, bf16[8,240,1024]{2,1,0:T(8,128)(2,1)} %coef_hbm.1, bf16[3,8,480,240]{3,2,1,0:T(8,128)(2,1)} %table_hbm.1, f32[8,240]{1,0:T(8,128)S(1)} %copy-done.1), custom_call_target="tpu_custom_call" | custom-call | flops 6000000000 | bytes 10000000 | tf_op jit(solution)/shard_map/move/pallas_call | solution.py:202
  11.7 3.6 %collective-permute-start = (f32[16,64,128]{2,1,0:T(8,128)S(1)}, f32[16,64,128]{2,1,0:T(8,128)S(1)}, u32[]{:S(2)}, u32[]{:S(2)}) collective-permute-start(f32[16,64,128]{2,1,0:T(8,128)S(1)} %get-tuple-element.32), channel_id=1, source_target_pairs={{0,1},{1,0},{2,3},{3,2},{4,5},{5,4},{6,7},{7,6},{8,9},{9,8},{10,11... | collective-permute-start | bytes 1572872 | tf_op jit(solution)/shard_map/ppermute | solution.py:430
  15.3 0.0 copy-done
  15.3 0.5 shard_map.86
  15.7 1.1 %collective-permute-done = f32[16,64,128]{2,1,0:T(8,128)S(1)} collective-permute-done((f32[16,64,128]{2,1,0:T(8,128)S(1)}, f32[16,64,128]{2,1,0:T(8,128)S(1)}, u32[]{:S(2)}, u32[]{:S(2)}) %collective-permute-start) | collective-permute-done | bytes 524320 | tf_op jit(solution)/shard_map/ppermute | solution.py:430
  16.8 0.9 %add.17 = f32[16,64,128]{2,1,0:T(8,128)} add(f32[16,64,128]{2,1,0:T(8,128)S(1)} %shard_map.86, f32[16,64,128]{2,1,0:T(8,128)S(1)} %collective-permute-done) | non-fusion elementwise | flops 131072 | bytes 1572864 | tf_op jit(solution)/shard_map/add | solution.py:438
  17.7 4.7 %all-to-all-start = ((f32[16,64,128]{2,1,0:T(8,128)}), f32[16,64,128]{2,1,0:T(8,128)S(1)}, u32[]{:S(2)}, u32[]{:S(2)}) async-start(f32[16,64,128]{2,1,0:T(8,128)} %add.17), calls=%async_computation | async-start | bytes 1048576 | tf_op jit(solution)/shard_map/all_to_all | solution.py:460
  22.4 0.1 pad_add_fusion.place_ref
  22.5 0.0 copy-done.3
  22.5 1.9 %shard_map.87 = (bf16[512,512]{1,0:T(8,128)(2,1)S(1)}, bf16[512,512]{1,0:T(8,128)(2,1)S(1)}, f32[2,128,128]{2,1,0:T(8,128)S(1)}, f32[2,128,128]{2,1,0:T(8,128)S(...) custom-call(s32[2]{0:T(128)S(1)} %pad_add_fusion.place_ref, f32[32,128]{1,0:T(8,128)S(1)} %copy-done.3), custom_call_target="tpu_custom_call" | custom-call | flops 100000000 | bytes 1654792 | tf_op jit(solution)/shard_map/pallas_call | solution.py:101
  24.4 1.1 %constant_dynamic-slice_fusion = (f32[240,32]{1,0:T(8,128)S(1)}, f32[240,32]{1,0:T(8,128)S(1)}) fusion(f32[240,1024]{1,0:T(8,128)} %param.11, s32[]{:T(128)S(6)} %select_n.7, s32[]{:T(128)S(6)} %select_n.6), kind=kLoop, calls=%fused_computation.2 | loop fusion | bytes 122888 | tf_op jit(solution)/shard_map/dynamic_slice | solution.py:457
  25.5 7.6 %all-to-all-done.got_ref = f32[16,64,128]{2,1,0:T(8,128)S(1)} async-done(((f32[16,64,128]{2,1,0:T(8,128)}), f32[16,64,128]{2,1,0:T(8,128)S(1)}, u32[]{:S(2)}, u32[]{:S(2)}) %all-to-all-start) | async-done | bytes 524320 | tf_op jit(solution)/shard_map/all_to_all | solution.py:460
  33.1 0.1 shard_map.88
  33.2 17.7 %all_to_all.15.line_ref = f32[8,72,128]{2,1,0:T(8,128)S(1)} all-to-all(f32[8,72,128]{2,1,0:T(8,128)S(1)} %shard_map.88), channel_id=1, replica_groups=mesh['sph_0'=4,'sph_1'=8,'ang_0'=4,'ang_1'=2] {'sph_1'}, dimensions={0} | all-to-all | bytes 589824 | tf_op jit(solution)/shard_map/all_to_all | solution.py:464
  50.9 4.2 %collective-permute-start.1 = (f32[64,128]{1,0:T(8,128)S(1)}, f32[64,128]{1,0:T(8,128)S(1)}, u32[]{:S(2)}, u32[]{:S(2)}) collective-permute-start(f32[64,128]{1,0:T(8,128)S(1)} %slice_reduce_fusion.own_ref), channel_id=1, source_target_pairs={{0,1},{1,0},{2,3},{3,2},{4,5},{5,4},{6,7},{7,6},{8,9},{9,8},{10,11... | collective-permute-start | bytes 98312 | tf_op jit(solution)/shard_map/ppermute | solution.py:466
  55.2 2.3 %shard_map.89.form_ref = f32[2,2,128,128]{3,2,1,0:T(8,128)S(1)} custom-call(f32[2,128,128]{2,1,0:T(8,128)S(1)} %get-tuple-element.51.radial_ref, f32[2,128,128]{2,1,0:T(8,128)S(1)} %get-tuple-element.52.scaled_ref, f32[8,72,128]{2,1,0:T(8,128)S(1)} %all_to_all.15.line_ref, f32[128,256]{1,0:T(8,128)S(1)} %get-tuple-element.53.waves_ref, ...), custom_call_target="tpu_custom_call" | custom-call | flops 1000000000 | bytes 1015808 | tf_op jit(solution)/shard_map/pallas_call | solution.py:101
  57.5 0.0 collective-permute-done.1.other_ref
  57.5 0.9 %shard_map.90 = f32[16,40,128]{2,1,0:T(8,128)S(1)} custom-call(s32[1]{0:T(128)} %bitcast.3.core_ref, f32[64,128]{1,0:T(8,128)S(1)} %slice_reduce_fusion.own_ref, f32[64,128]{1,0:T(8,128)S(1)} %collective-permute-done.1.other_ref, bf16[512,512]{1,0:T(8,128)(2,1)S(1)} %get-tuple-element.49.high_ref, bf16[512,512]{1,0:T(8,128)(2,1)S(1)} %get-tuple-element.50.low_ref, ...), custom_call_target="tpu_custom_call" | custom-call | flops 400000000 | bytes 1896452 | tf_op jit(solution)/shard_map/pallas_call | solution.py:101
  58.4 12.3 %all_to_all.16.got_ref = f32[16,40,128]{2,1,0:T(8,128)S(1)} all-to-all(f32[16,40,128]{2,1,0:T(8,128)S(1)} %shard_map.90), channel_id=1, replica_groups=mesh['sph_0'=4,'sph_1'=8,'ang_0'=4,'ang_1'=2] {'ang_0','sph_0'}, dimensions={0} | all-to-all | bytes 655360 | tf_op jit(solution)/shard_map/all_to_all | solution.py:480
  70.7 1.0 %shard_map.91 = (f32[4,32,512]{2,1,0:T(8,128)}, f32[3,64]{1,0:T(4,128)}) custom-call(s32[1]{0:T(128)} %bitcast.4.place_ref, f32[16,40,128]{2,1,0:T(8,128)S(1)} %all_to_all.16.got_ref), custom_call_target="tpu_custom_call" | custom-call | flops 1 | bytes 590596 | tf_op jit(solution)/shard_map/pallas_call | solution.py:101
  (1 shorter events, 0.0 us)
Async XLA Ops:
  0.6 0.7 copy-start.1
  1.3 0.7 copy-start.2
  2.0 13.2 %copy-start = (f32[4,64]{1,0:T(4,128)S(1)}, f32[4,64]{1,0:T(4,128)}, u32[]{:S(2)}) copy-start(f32[4,64]{1,0:T(4,128)} %detector_ref.1) | copy-start | bytes 3076
  2.0 20.5 %copy-start.3 = (f32[32,128]{1,0:T(8,128)S(1)}, f32[32,128]{1,0:T(8,128)}, u32[]{:S(2)}) copy-start(f32[32,128]{1,0:T(8,128)} %constant.34.clone.const_ref) | copy-start | bytes 49156
  11.7 5.1 %collective-permute-start = (f32[16,64,128]{2,1,0:T(8,128)S(1)}, f32[16,64,128]{2,1,0:T(8,128)S(1)}, u32[]{:S(2)}, u32[]{:S(2)}) collective-permute-start(f32[16,64,128]{2,1,0:T(8,128)S(1)} %get-tuple-element.32), channel_id=1, source_target_pairs={{0,1},{1,0},{2,3},{3,2},{4,5},{5,4},{6,7},{7,6},{8,9},{9,8},{10,11... | collective-permute-start | bytes 1572872 | tf_op jit(solution)/shard_map/ppermute | solution.py:430
  17.7 15.5 %all-to-all-start = ((f32[16,64,128]{2,1,0:T(8,128)}), f32[16,64,128]{2,1,0:T(8,128)S(1)}, u32[]{:S(2)}, u32[]{:S(2)}) async-start(f32[16,64,128]{2,1,0:T(8,128)} %add.17), calls=%async_computation | async-start | bytes 1048576 | tf_op jit(solution)/shard_map/all_to_all | solution.py:460
  50.9 6.5 %collective-permute-start.1 = (f32[64,128]{1,0:T(8,128)S(1)}, f32[64,128]{1,0:T(8,128)S(1)}, u32[]{:S(2)}, u32[]{:S(2)}) collective-permute-start(f32[64,128]{1,0:T(8,128)S(1)} %slice_reduce_fusion.own_ref), channel_id=1, source_target_pairs={{0,1},{1,0},{2,3},{3,2},{4,5},{5,4},{6,7},{7,6},{8,9},{9,8},{10,11... | collective-permute-start | bytes 98312 | tf_op jit(solution)/shard_map/ppermute | solution.py:466

commit v5 on v4

--- a/solution.py
+++ b/solution.py
@@ -155,12 +155,12 @@
     absorbed[...] = jnp.zeros_like(absorbed)
     weights = weight_ref[...].T
     for group in range(groups):
+        for copy in first if group == 0 else first + second:
+            copy.wait()
         if group + 1 < groups:
             ahead = fetches(group + 1)
             for copy in ahead[0] + ahead[1]:
                 copy.start()
-        for copy in first if group == 0 else first + second:
-            copy.wait()
         for s in range(unroll):
             j = group * unroll + s
             real, imag = coef[j, :, :FIELDS].astype(F32), coef[j, :, FIELDS:].astype(F32)
@@ -235,7 +235,7 @@
 
 
 def tables_kernel(
-    place_ref, const_ref, high_ref, low_ref, whole_ref, scaled_ref, gap_ref, waves_ref, phase_ref
+    place_ref, const_ref, high_ref, low_ref, turned_ref, fixed_ref, gap_ref, waves_ref, phase_ref
 ):
     z, core = place_ref[0], place_ref[1]
     row = lambda shape: lax.broadcasted_iota(jnp.int32, shape, 0)
@@ -261,8 +261,11 @@
     )
     weight = sine_theta * (2.0 * math.pi * math.pi / (POLAR * AZIM))
     for sign, table in enumerate((plus, minus)):
-        whole_ref[sign] = table
-        scaled_ref[sign] = table * weight
+        turned_ref[sign] = (table * weight).T
+        high, low = halves(table)
+        for block in range(2):
+            fixed_ref[sign, block * LANES : (block + 1) * LANES, :LANES] = high
+            fixed_ref[sign, block * LANES : (block + 1) * LANES, LANES:] = low
 
     across = lambda r: jnp.broadcast_to(const_ref[r : r + 1], (LANES, LANES))
     used = across(1) > 0
@@ -281,7 +284,7 @@
         waves_ref[:, half * LANES : (half + 1) * LANES] = wave
 
 
-def power_kernel(radial_ref, scaled_ref, line_ref, waves_ref, gap_ref, out_ref):
+def power_kernel(turned_ref, fixed_ref, line_ref, waves_ref, gap_ref, out_ref):
     gap = gap_ref[...]
     detectors = line_ref[:, 64:].reshape(64, LANES)
     group = lax.broadcasted_iota(jnp.int32, detectors.shape, 1) // CHUNK
@@ -295,10 +298,8 @@
     far = jnp.abs(gap[:HALF])
     far = jnp.concatenate([far, far], axis=0)
     for sign in range(2):
-        table = scaled_ref[sign].T[:HALF]
-        high, low = halves(radial_ref[sign])
-        fixed = jnp.concatenate([high, low], axis=1)
-        fixed = jnp.concatenate([fixed, fixed], axis=0)
+        table = turned_ref[sign, :HALF]
+        fixed = fixed_ref[sign]
         total = jnp.zeros((COEFS, LANES), F32)
         for start in range(0, 2 * ORDER + 1, 7):
             rows = []
@@ -439,11 +440,11 @@
     packed, incident, x, z, y, core = lax.optimization_barrier(
         (packed, incident, x, z, y, core)
     )
-    high, low, whole, scaled, gap, waves, phase = call(
+    high, low, turned, fixed, gap, waves, phase = call(
         tables_kernel,
         [
             struct((2 * ROWS, 2 * ROWS), BF16), struct((2 * ROWS, 2 * ROWS), BF16),
-            struct((2, POLAR, LANES)), struct((2, POLAR, LANES)), struct((LANES, LANES)),
+            struct((2, LANES, POLAR)), struct((2, 2 * POLAR, 2 * LANES), BF16), struct((LANES, LANES)),
             struct((LANES, 2 * LANES)), struct((2, LANES, LANES)),
         ],
         [jnp.stack([z, core]), jnp.asarray(constants())],
@@ -452,14 +453,14 @@
     )
     first = (4 * y + x) * CHUNK
     tables = (
-        whole, scaled, waves, gap, high, low, phase,
+        turned, fixed, waves, gap, high, low, phase,
         lax.dynamic_slice_in_dim(incident, first, CHUNK, 1),
         lax.dynamic_slice_in_dim(incident, FIELDS + first, CHUNK, 1),
         core.astype(jnp.int32).reshape(1), (4 * y + 2 * core).astype(jnp.int32).reshape(1),
     )
     got = lax.all_to_all(packed, PLANE, 0, 0, tiled=True)
     got, tables = lax.optimization_barrier((got, tables))
-    whole, scaled, waves, gap, high, low, phase, inc_real, inc_imag, core, place = tables
+    turned, fixed, waves, gap, high, low, phase, inc_real, inc_imag, core, place = tables
     (spread,) = call(plane_kernel, [struct((8, 72, LANES))], [got])
     line = lax.all_to_all(spread, LINE, 0, 0, tiled=True)
     own = line[:, :64].sum(axis=0)
@@ -467,7 +468,7 @@
     (form,) = call(
         power_kernel,
         [struct((2, 2, LANES, LANES))],
-        [whole, scaled, line, waves, gap],
+        [turned, fixed, line, waves, gap],
         flops=1_000_000_000,
     )
     (messages,) = call(

time: 72 us -> 71.9 us (level)
  no operation moved by 1% of the time
where the time goes in v5:
time: 71.9 us; the launch traced here: 71.5 us
  blocking collectives  29.8 us (41%)
  Pallas kernels  16.4 us (23%)
  starting transfers between devices  12.6 us (18%)
  waiting for transfers between devices  8.59 us (12%)
  local copies, waits for them, and re-layouts  2.47 us (3%)
  other arithmetic  0.96 us (1%)
  between operations  0.73 us (1%)
    all_to_all x1, blocking collectives, shards(): line = lax.all_to_all(spread, LINE, 0, 0, tiled=True)  17.6 us
    all_to_all x1, blocking collectives, shards(): got = lax.all_to_all(messages, PLANE, 0, 0, tiled=True)  12.3 us
    pallas_call x1, Pallas kernels, moved_sum(): pl.pallas_call(functools.partial(move_kernel, unroll), in_specs=[smem, sm...  9.64 us
    all_to_all x1, waiting for transfers between devices, shards(): got = lax.all_to_all(packed, PLANE, 0, 0, tiled=True)  7.54 us
    pallas_call x6, Pallas kernels, call(): pl.pallas_call(body, out_shape=[jax.ShapeDtypeStruct(o.shape, o.dtype) fo...  6.72 us
    all_to_all x1, starting transfers between devices, shards(): got = lax.all_to_all(packed, PLANE, 0, 0, tiled=True)  4.87 us
    ppermute x1, starting transfers between devices, shards(): partner = lax.ppermute(own, PAIR, [(0, 1), (1, 0)])  4.25 us
    ppermute x1, starting transfers between devices, shards(): other = lax.ppermute(theirs, PAIR, [(0, 1), (1, 0)])  3.45 us
  transfers between devices with their start and end apart: 3, of which 2 were waited for; matrix products, arithmetic and copies ran while one was open for 2% of the time, Pallas kernels for 7%

profile of v5, /device:TPU:1, one launch (start us, length us, event | category | flops | bytes accessed | tf_op | source)
XLA Modules:
  0.0 71.5 jit_solution(5425244922682535008)
XLA Ops:
  0.6 0.0 copy-start.1
  0.6 0.7 copy-done.1
  1.3 0.0 copy-start.2
  1.3 0.7 copy-done.2
  2.0 0.0 copy-start
  2.0 0.0 copy-start.3
  2.0 9.6 %move.1 = (f32[2,256,512]{2,1,0:T(8,128)S(1)}, f32[16,64,128]{2,1,0:T(8,128)S(1)}) custom-call(s32[1]{0:T(128)} %bitcast.core_ref, s32[3,8]{1,0:T(4,128)S(1)} %bitcast.6, bf16[8,240,1024]{2,1,0:T(8,128)(2,1)} %coef_hbm.1, bf16[3,8,480,240]{3,2,1,0:T(8,128)(2,1)} %table_hbm.1, f32[8,240]{1,0:T(8,128)S(1)} %copy-done.1), custom_call_target="tpu_custom_call" | custom-call | flops 6000000000 | bytes 10000000 | tf_op jit(solution)/shard_map/move/pallas_call | solution.py:202
  11.7 3.5 %collective-permute-start = (f32[16,64,128]{2,1,0:T(8,128)S(1)}, f32[16,64,128]{2,1,0:T(8,128)S(1)}, u32[]{:S(2)}, u32[]{:S(2)}) collective-permute-start(f32[16,64,128]{2,1,0:T(8,128)S(1)} %get-tuple-element.32), channel_id=1, source_target_pairs={{0,1},{1,0},{2,3},{3,2},{4,5},{5,4},{6,7},{7,6},{8,9},{9,8},{10,11... | collective-permute-start | bytes 1572872 | tf_op jit(solution)/shard_map/ppermute | solution.py:431
  15.1 0.0 copy-done
  15.1 0.5 shard_map.86
  15.6 1.1 %collective-permute-done = f32[16,64,128]{2,1,0:T(8,128)S(1)} collective-permute-done((f32[16,64,128]{2,1,0:T(8,128)S(1)}, f32[16,64,128]{2,1,0:T(8,128)S(1)}, u32[]{:S(2)}, u32[]{:S(2)}) %collective-permute-start) | collective-permute-done | bytes 524320 | tf_op jit(solution)/shard_map/ppermute | solution.py:431
  16.7 0.9 %add.17 = f32[16,64,128]{2,1,0:T(8,128)} add(f32[16,64,128]{2,1,0:T(8,128)S(1)} %shard_map.86, f32[16,64,128]{2,1,0:T(8,128)S(1)} %collective-permute-done) | non-fusion elementwise | flops 131072 | bytes 1572864 | tf_op jit(solution)/shard_map/add | solution.py:439
  17.5 4.9 %all-to-all-start = ((f32[16,64,128]{2,1,0:T(8,128)}), f32[16,64,128]{2,1,0:T(8,128)S(1)}, u32[]{:S(2)}, u32[]{:S(2)}) async-start(f32[16,64,128]{2,1,0:T(8,128)} %add.17), calls=%async_computation | async-start | bytes 1048576 | tf_op jit(solution)/shard_map/all_to_all | solution.py:461
  22.4 0.1 pad_add_fusion.place_ref
  22.5 0.0 copy-done.3
  22.5 2.0 %shard_map.87 = (bf16[512,512]{1,0:T(8,128)(2,1)S(1)}, bf16[512,512]{1,0:T(8,128)(2,1)S(1)}, f32[2,128,128]{2,1,0:T(8,128)S(1)}, bf16[2,256,256]{2,1,0:T(8,128)(...) custom-call(s32[2]{0:T(128)S(1)} %pad_add_fusion.place_ref, ...), custom_call_target="tpu_custom_call" | custom-call | flops 100000000 | bytes 1785864 | tf_op jit(solution)/shard_map/pallas_call | solution.py:101
  24.5 1.1 %constant_dynamic-slice_fusion = (f32[240,32]{1,0:T(8,128)S(1)}, f32[240,32]{1,0:T(8,128)S(1)}) fusion(f32[240,1024]{1,0:T(8,128)} %param.11, s32[]{:T(128)S(6)} %select_n.7, s32[]{:T(128)S(6)} %select_n.6), kind=kLoop, calls=%fused_computation.2 | loop fusion | bytes 122888 | tf_op jit(solution)/shard_map/dynamic_slice | solution.py:458
  25.6 7.5 %all-to-all-done.got_ref = f32[16,64,128]{2,1,0:T(8,128)S(1)} async-done(((f32[16,64,128]{2,1,0:T(8,128)}), f32[16,64,128]{2,1,0:T(8,128)S(1)}, u32[]{:S(2)}, u32[]{:S(2)}) %all-to-all-start) | async-done | bytes 524320 | tf_op jit(solution)/shard_map/all_to_all | solution.py:461
  33.1 0.1 shard_map.88
  33.2 17.6 %all_to_all.15.line_ref = f32[8,72,128]{2,1,0:T(8,128)S(1)} all-to-all(f32[8,72,128]{2,1,0:T(8,128)S(1)} %shard_map.88), channel_id=1, replica_groups=mesh['sph_0'=4,'sph_1'=8,'ang_0'=4,'ang_1'=2] {'sph_1'}, dimensions={0} | all-to-all | bytes 589824 | tf_op jit(solution)/shard_map/all_to_all | solution.py:465
  50.8 4.2 %collective-permute-start.1 = (f32[64,128]{1,0:T(8,128)S(1)}, f32[64,128]{1,0:T(8,128)S(1)}, u32[]{:S(2)}, u32[]{:S(2)}) collective-permute-start(f32[64,128]{1,0:T(8,128)S(1)} %slice_reduce_fusion.own_ref), channel_id=1, source_target_pairs={{0,1},{1,0},{2,3},{3,2},{4,5},{5,4},{6,7},{7,6},{8,9},{9,8},{10,11... | collective-permute-start | bytes 98312 | tf_op jit(solution)/shard_map/ppermute | solution.py:467
  55.0 2.3 %shard_map.89.form_ref = f32[2,2,128,128]{3,2,1,0:T(8,128)S(1)} custom-call(f32[2,128,128]{2,1,0:T(8,128)S(1)} %get-tuple-element.51.turned_ref, bf16[2,256,256]{2,1,0:T(8,128)(2,1)S(1)} %get-tuple-element.52.fixed_ref, f32[8,72,128]{2,1,0:T(8,128)S(1)} %all_to_all.15.line_ref, f32[128,256]{1,0:T(8,128)S(1)} %get-tuple-element.53.waves_ref, ...), custom_call_target="tpu_custom_call" | custom-call | flops 1000000000 | bytes 1146880 | tf_op jit(solution)/shard_map/pallas_call | solution.py:101
  57.3 0.0 collective-permute-done.1.other_ref
  57.3 0.9 %shard_map.90 = f32[16,40,128]{2,1,0:T(8,128)S(1)} custom-call(s32[1]{0:T(128)} %bitcast.3.core_ref, f32[64,128]{1,0:T(8,128)S(1)} %slice_reduce_fusion.own_ref, f32[64,128]{1,0:T(8,128)S(1)} %collective-permute-done.1.other_ref, bf16[512,512]{1,0:T(8,128)(2,1)S(1)} %get-tuple-element.49.high_ref, bf16[512,512]{1,0:T(8,128)(2,1)S(1)} %get-tuple-element.50.low_ref, ...), custom_call_target="tpu_custom_call" | custom-call | flops 400000000 | bytes 1896452 | tf_op jit(solution)/shard_map/pallas_call | solution.py:101
  58.3 12.3 %all_to_all.16.got_ref = f32[16,40,128]{2,1,0:T(8,128)S(1)} all-to-all(f32[16,40,128]{2,1,0:T(8,128)S(1)} %shard_map.90), channel_id=1, replica_groups=mesh['sph_0'=4,'sph_1'=8,'ang_0'=4,'ang_1'=2] {'ang_0','sph_0'}, dimensions={0} | all-to-all | bytes 655360 | tf_op jit(solution)/shard_map/all_to_all | solution.py:481
  70.5 1.0 %shard_map.91 = (f32[4,32,512]{2,1,0:T(8,128)}, f32[3,64]{1,0:T(4,128)}) custom-call(s32[1]{0:T(128)} %bitcast.4.place_ref, f32[16,40,128]{2,1,0:T(8,128)S(1)} %all_to_all.16.got_ref), custom_call_target="tpu_custom_call" | custom-call | flops 1 | bytes 590596 | tf_op jit(solution)/shard_map/pallas_call | solution.py:101
  (1 shorter events, 0.0 us)
Async XLA Ops:
  0.6 0.7 copy-start.1
  1.3 0.7 copy-start.2
  2.0 13.1 %copy-start = (f32[4,64]{1,0:T(4,128)S(1)}, f32[4,64]{1,0:T(4,128)}, u32[]{:S(2)}) copy-start(f32[4,64]{1,0:T(4,128)} %detector_ref.1) | copy-start | bytes 3076
  2.0 20.5 %copy-start.3 = (f32[32,128]{1,0:T(8,128)S(1)}, f32[32,128]{1,0:T(8,128)}, u32[]{:S(2)}) copy-start(f32[32,128]{1,0:T(8,128)} %constant.34.clone.const_ref) | copy-start | bytes 49156
  11.7 5.0 %collective-permute-start = (f32[16,64,128]{2,1,0:T(8,128)S(1)}, f32[16,64,128]{2,1,0:T(8,128)S(1)}, u32[]{:S(2)}, u32[]{:S(2)}) collective-permute-start(f32[16,64,128]{2,1,0:T(8,128)S(1)} %get-tuple-element.32), channel_id=1, source_target_pairs={{0,1},{1,0},{2,3},{3,2},{4,5},{5,4},{6,7},{7,6},{8,9},{9,8},{10,11... | collective-permute-start | bytes 1572872 | tf_op jit(solution)/shard_map/ppermute | solution.py:431
  17.5 15.6 %all-to-all-start = ((f32[16,64,128]{2,1,0:T(8,128)}), f32[16,64,128]{2,1,0:T(8,128)S(1)}, u32[]{:S(2)}, u32[]{:S(2)}) async-start(f32[16,64,128]{2,1,0:T(8,128)} %add.17), calls=%async_computation | async-start | bytes 1048576 | tf_op jit(solution)/shard_map/all_to_all | solution.py:461
  50.8 6.5 %collective-permute-start.1 = (f32[64,128]{1,0:T(8,128)S(1)}, f32[64,128]{1,0:T(8,128)S(1)}, u32[]{:S(2)}, u32[]{:S(2)}) collective-permute-start(f32[64,128]{1,0:T(8,128)S(1)} %slice_reduce_fusion.own_ref), channel_id=1, source_target_pairs={{0,1},{1,0},{2,3},{3,2},{4,5},{5,4},{6,7},{7,6},{8,9},{9,8},{10,11... | collective-permute-start | bytes 98312 | tf_op jit(solution)/shard_map/ppermute | solution.py:467

commit v6 on v5

--- a/solution.py
+++ b/solution.py
@@ -128,8 +128,8 @@
 
 
 def move_kernel(
-    unroll, core_ref, cell_ref, coef_hbm, table_hbm, weight_ref, total, theirs_ref,
-    coef, table, absorbed, right, sems,
+    unroll, core_ref, coef_hbm, table_hbm, weight_ref, total, theirs_ref,
+    coef, table, absorbed, right, cell_ref, sems, cell_sem,
 ):
     spheres = coef.shape[0]
     groups = spheres // unroll
@@ -140,7 +140,9 @@
     def table_copy(j, stage):
         axis = 2 - stage
         return pltpu.make_async_copy(
-            table_hbm.at[axis, cell_ref[axis, j]], table.at[stage, j], sems.at[stage, j]
+            table_hbm.at[axis, cell_ref[spheres + axis, j].astype(jnp.int32)],
+            table.at[stage, j],
+            sems.at[stage, j],
         )
 
     def fetches(group):
@@ -148,12 +150,17 @@
         first = [copy for j in own for copy in (coef_copy(j), table_copy(j, 0))]
         return first, [table_copy(j, stage) for stage in (1, 2) for j in own]
 
+    for j in range(unroll):
+        coef_copy(j).start()
+    cells = pltpu.make_async_copy(weight_ref, cell_ref, cell_sem)
+    cells.start()
+    cells.wait()
     first, second = fetches(0)
-    for copy in first + second:
+    for copy in first[1::2] + second:
         copy.start()
     total[...] = jnp.zeros_like(total)
     absorbed[...] = jnp.zeros_like(absorbed)
-    weights = weight_ref[...].T
+    weights = weight_ref[:spheres].T[:COEFS]
     for group in range(groups):
         for copy in first if group == 0 else first + second:
             copy.wait()
@@ -197,18 +204,28 @@
 def moved_sum(coefficients, positions, shift_tables, absorb_weight, core, unroll=2):
     spheres = coefficients.shape[0]
     smem = pl.BlockSpec(memory_space=pltpu.SMEM)
+    cells = positions.T.astype(F32)
+    weights = jnp.concatenate(
+        [
+            jnp.pad(absorb_weight, ((0, 0), (0, ROWS - COEFS))),
+            jnp.pad(cells, ((0, 8 - cells.shape[0]), (0, ROWS - spheres))),
+        ],
+        axis=0,
+    )
     hbm = pl.BlockSpec(memory_space=pltpu.HBM)
     vmem = pl.BlockSpec(memory_space=pltpu.VMEM)
     return pl.pallas_call(
         functools.partial(move_kernel, unroll),
-        in_specs=[smem, smem, hbm, hbm, vmem],
+        in_specs=[smem, hbm, hbm, vmem],
         out_specs=[vmem, vmem],
         scratch_shapes=[
             pltpu.VMEM((spheres, COEFS, 2 * FIELDS), BF16),
             pltpu.VMEM((3, spheres, 2 * COEFS, COEFS), BF16),
             pltpu.VMEM((8, FIELDS), F32),
             pltpu.VMEM((unroll, 2 * ROWS, FIELDS), BF16),
+            pltpu.SMEM((spheres + 8, ROWS), F32),
             pltpu.SemaphoreType.DMA((4, spheres)),
+            pltpu.SemaphoreType.DMA,
         ],
         out_shape=[struct((2, ROWS, FIELDS)), struct((16, 64, LANES))],
         compiler_params=pltpu.CompilerParams(vmem_limit_bytes=52 * 1024 * 1024),
@@ -216,7 +233,7 @@
             flops=6_000_000_000, bytes_accessed=10_000_000, transcendentals=0
         ),
         name="move",
-    )(core, positions.T, coefficients, shift_tables, absorb_weight)
+    )(core, coefficients, shift_tables, weights)
 
 
 def plane_kernel(got_ref, out_ref):

time: 71.9 us -> 71.9 us (level)
  other arithmetic: 0.96 us -> 2.33 us
  local copies, waits for them, and re-layouts: 2.47 us -> 1.1 us
    unnamed x8 -> x4, local copies, waits for them, and re-layouts: 1.38 us -> 0.01 us
where the time goes in v6:
time: 71.9 us; the launch traced here: 71.5 us
  blocking collectives  29.8 us (41%)
  Pallas kernels  16.3 us (23%)
  starting transfers between devices  12.6 us (18%)
  waiting for transfers between devices  8.59 us (12%)
  other arithmetic  2.33 us (3%)
  local copies, waits for them, and re-layouts  1.1 us (2%)
  between operations  0.72 us (1%)
    all_to_all x1, blocking collectives, shards(): line = lax.all_to_all(spread, LINE, 0, 0, tiled=True)  17.5 us
    all_to_all x1, blocking collectives, shards(): got = lax.all_to_all(messages, PLANE, 0, 0, tiled=True)  12.3 us
    pallas_call x1, Pallas kernels, moved_sum(): pl.pallas_call(functools.partial(move_kernel, unroll), in_specs=[smem, hb...  9.61 us
    all_to_all x1, waiting for transfers between devices, shards(): got = lax.all_to_all(packed, PLANE, 0, 0, tiled=True)  7.54 us
    pallas_call x6, Pallas kernels, call(): pl.pallas_call(body, out_shape=[jax.ShapeDtypeStruct(o.shape, o.dtype) fo...  6.72 us
    all_to_all x1, starting transfers between devices, shards(): got = lax.all_to_all(packed, PLANE, 0, 0, tiled=True)  5.03 us
    ppermute x1, starting transfers between devices, shards(): partner = lax.ppermute(own, PAIR, [(0, 1), (1, 0)])  4.25 us
    ppermute x1, starting transfers between devices, shards(): other = lax.ppermute(theirs, PAIR, [(0, 1), (1, 0)])  3.31 us
  transfers between devices with their start and end apart: 3, of which 2 were waited for; matrix products, arithmetic and copies ran while one was open for 2% of the time, Pallas kernels for 7%

profile of v6, /device:TPU:1, one launch (start us, length us, event | category | flops | bytes accessed | tf_op | source)
XLA Modules:
  0.0 71.5 jit_solution(1331158645903144164)
XLA Ops:
  0.6 0.7 convert_bitcast_fusion
  1.3 0.7 select_maximum_fusion.weight_ref
  2.0 0.0 copy-start
  2.0 0.0 copy-start.1
  2.0 9.6 %move.1 = (f32[2,256,512]{2,1,0:T(8,128)S(1)}, f32[16,64,128]{2,1,0:T(8,128)S(1)}) custom-call(s32[1]{0:T(128)} %bitcast.core_ref, bf16[8,240,1024]{2,1,0:T(8,128)(2,1)} %coef_hbm.1, bf16[3,8,480,240]{3,2,1,0:T(8,128)(2,1)} %table_hbm.1, f32[16,256]{1,0:T(8,128)S(1)} %select_maximum_fusion.weight_ref), custom_call_target="tpu_custom_call" | custom-call | flops 6000000000 | bytes 10000000 | tf_op jit(solution)/shard_map/move/pallas_call | solution.py:217
  11.6 3.3 %collective-permute-start = (f32[16,64,128]{2,1,0:T(8,128)S(1)}, f32[16,64,128]{2,1,0:T(8,128)S(1)}, u32[]{:S(2)}, u32[]{:S(2)}) collective-permute-start(f32[16,64,128]{2,1,0:T(8,128)S(1)} %get-tuple-element.32), channel_id=1, source_target_pairs={{0,1},{1,0},{2,3},{3,2},{4,5},{5,4},{6,7},{7,6},{8,9},{9,8},{10,11... | collective-permute-start | bytes 1572872 | tf_op jit(solution)/shard_map/ppermute | solution.py:448
  15.0 0.0 copy-done
  15.0 0.5 shard_map.86
  15.4 1.1 %collective-permute-done = f32[16,64,128]{2,1,0:T(8,128)S(1)} collective-permute-done((f32[16,64,128]{2,1,0:T(8,128)S(1)}, f32[16,64,128]{2,1,0:T(8,128)S(1)}, u32[]{:S(2)}, u32[]{:S(2)}) %collective-permute-start) | collective-permute-done | bytes 524320 | tf_op jit(solution)/shard_map/ppermute | solution.py:448
  16.5 0.9 %add.21 = f32[16,64,128]{2,1,0:T(8,128)} add(f32[16,64,128]{2,1,0:T(8,128)S(1)} %shard_map.86, f32[16,64,128]{2,1,0:T(8,128)S(1)} %collective-permute-done) | non-fusion elementwise | flops 131072 | bytes 1572864 | tf_op jit(solution)/shard_map/add | solution.py:456
  17.3 5.0 %all-to-all-start = ((f32[16,64,128]{2,1,0:T(8,128)}), f32[16,64,128]{2,1,0:T(8,128)S(1)}, u32[]{:S(2)}, u32[]{:S(2)}) async-start(f32[16,64,128]{2,1,0:T(8,128)} %add.21), calls=%async_computation | async-start | bytes 1048576 | tf_op jit(solution)/shard_map/all_to_all | solution.py:478
  22.4 0.1 pad_add_fusion.place_ref
  22.5 0.0 copy-done.1
  22.5 2.0 %shard_map.87 = (bf16[512,512]{1,0:T(8,128)(2,1)S(1)}, bf16[512,512]{1,0:T(8,128)(2,1)S(1)}, f32[2,128,128]{2,1,0:T(8,128)S(1)}, bf16[2,256,256]{2,1,0:T(8,128)(...) custom-call(s32[2]{0:T(128)S(1)} %pad_add_fusion.place_ref, ...), custom_call_target="tpu_custom_call" | custom-call | flops 100000000 | bytes 1785864 | tf_op jit(solution)/shard_map/pallas_call | solution.py:101
  24.5 1.1 %constant_dynamic-slice_fusion = (f32[240,32]{1,0:T(8,128)S(1)}, f32[240,32]{1,0:T(8,128)S(1)}) fusion(f32[240,1024]{1,0:T(8,128)} %param.11, s32[]{:T(128)S(6)} %select_n.7, s32[]{:T(128)S(6)} %select_n.6), kind=kLoop, calls=%fused_computation.6 | loop fusion | bytes 122888 | tf_op jit(solution)/shard_map/dynamic_slice | solution.py:475
  25.6 7.5 %all-to-all-done.got_ref = f32[16,64,128]{2,1,0:T(8,128)S(1)} async-done(((f32[16,64,128]{2,1,0:T(8,128)}), f32[16,64,128]{2,1,0:T(8,128)S(1)}, u32[]{:S(2)}, u32[]{:S(2)}) %all-to-all-start) | async-done | bytes 524320 | tf_op jit(solution)/shard_map/all_to_all | solution.py:478
  33.1 0.1 shard_map.88
  33.2 17.5 %all_to_all.15.line_ref = f32[8,72,128]{2,1,0:T(8,128)S(1)} all-to-all(f32[8,72,128]{2,1,0:T(8,128)S(1)} %shard_map.88), channel_id=1, replica_groups=mesh['sph_0'=4,'sph_1'=8,'ang_0'=4,'ang_1'=2] {'sph_1'}, dimensions={0} | all-to-all | bytes 589824 | tf_op jit(solution)/shard_map/all_to_all | solution.py:482
  50.7 4.2 %collective-permute-start.1 = (f32[64,128]{1,0:T(8,128)S(1)}, f32[64,128]{1,0:T(8,128)S(1)}, u32[]{:S(2)}, u32[]{:S(2)}) collective-permute-start(f32[64,128]{1,0:T(8,128)S(1)} %slice_reduce_fusion.own_ref), channel_id=1, source_target_pairs={{0,1},{1,0},{2,3},{3,2},{4,5},{5,4},{6,7},{7,6},{8,9},{9,8},{10,11... | collective-permute-start | bytes 98312 | tf_op jit(solution)/shard_map/ppermute | solution.py:484
  55.0 2.3 %shard_map.89.form_ref = f32[2,2,128,128]{3,2,1,0:T(8,128)S(1)} custom-call(f32[2,128,128]{2,1,0:T(8,128)S(1)} %get-tuple-element.51.turned_ref, bf16[2,256,256]{2,1,0:T(8,128)(2,1)S(1)} %get-tuple-element.52.fixed_ref, f32[8,72,128]{2,1,0:T(8,128)S(1)} %all_to_all.15.line_ref, f32[128,256]{1,0:T(8,128)S(1)} %get-tuple-element.53.waves_ref, ...), custom_call_target="tpu_custom_call" | custom-call | flops 1000000000 | bytes 1146880 | tf_op jit(solution)/shard_map/pallas_call | solution.py:101
  57.3 0.0 collective-permute-done.1.other_ref
  57.3 0.9 %shard_map.90 = f32[16,40,128]{2,1,0:T(8,128)S(1)} custom-call(s32[1]{0:T(128)} %bitcast.3.core_ref, f32[64,128]{1,0:T(8,128)S(1)} %slice_reduce_fusion.own_ref, f32[64,128]{1,0:T(8,128)S(1)} %collective-permute-done.1.other_ref, bf16[512,512]{1,0:T(8,128)(2,1)S(1)} %get-tuple-element.49.high_ref, bf16[512,512]{1,0:T(8,128)(2,1)S(1)} %get-tuple-element.50.low_ref, ...), custom_call_target="tpu_custom_call" | custom-call | flops 400000000 | bytes 1896452 | tf_op jit(solution)/shard_map/pallas_call | solution.py:101
  58.2 12.3 %all_to_all.16.got_ref = f32[16,40,128]{2,1,0:T(8,128)S(1)} all-to-all(f32[16,40,128]{2,1,0:T(8,128)S(1)} %shard_map.90), channel_id=1, replica_groups=mesh['sph_0'=4,'sph_1'=8,'ang_0'=4,'ang_1'=2] {'ang_0','sph_0'}, dimensions={0} | all-to-all | bytes 655360 | tf_op jit(solution)/shard_map/all_to_all | solution.py:498
  70.5 1.0 %shard_map.91 = (f32[4,32,512]{2,1,0:T(8,128)}, f32[3,64]{1,0:T(4,128)}) custom-call(s32[1]{0:T(128)} %bitcast.4.place_ref, f32[16,40,128]{2,1,0:T(8,128)S(1)} %all_to_all.16.got_ref), custom_call_target="tpu_custom_call" | custom-call | flops 1 | bytes 590596 | tf_op jit(solution)/shard_map/pallas_call | solution.py:101
  (1 shorter events, 0.0 us)
Async XLA Ops:
  2.0 12.9 %copy-start = (f32[4,64]{1,0:T(4,128)S(1)}, f32[4,64]{1,0:T(4,128)}, u32[]{:S(2)}) copy-start(f32[4,64]{1,0:T(4,128)} %detector_ref.1) | copy-start | bytes 3076
  2.0 20.5 %copy-start.1 = (f32[32,128]{1,0:T(8,128)S(1)}, f32[32,128]{1,0:T(8,128)}, u32[]{:S(2)}) copy-start(f32[32,128]{1,0:T(8,128)} %constant.35.clone.const_ref) | copy-start | bytes 49156
  11.6 4.8 %collective-permute-start = (f32[16,64,128]{2,1,0:T(8,128)S(1)}, f32[16,64,128]{2,1,0:T(8,128)S(1)}, u32[]{:S(2)}, u32[]{:S(2)}) collective-permute-start(f32[16,64,128]{2,1,0:T(8,128)S(1)} %get-tuple-element.32), channel_id=1, source_target_pairs={{0,1},{1,0},{2,3},{3,2},{4,5},{5,4},{6,7},{7,6},{8,9},{9,8},{10,11... | collective-permute-start | bytes 1572872 | tf_op jit(solution)/shard_map/ppermute | solution.py:448
  17.3 15.8 %all-to-all-start = ((f32[16,64,128]{2,1,0:T(8,128)}), f32[16,64,128]{2,1,0:T(8,128)S(1)}, u32[]{:S(2)}, u32[]{:S(2)}) async-start(f32[16,64,128]{2,1,0:T(8,128)} %add.21), calls=%async_computation | async-start | bytes 1048576 | tf_op jit(solution)/shard_map/all_to_all | solution.py:478
  50.7 6.5 %collective-permute-start.1 = (f32[64,128]{1,0:T(8,128)S(1)}, f32[64,128]{1,0:T(8,128)S(1)}, u32[]{:S(2)}, u32[]{:S(2)}) collective-permute-start(f32[64,128]{1,0:T(8,128)S(1)} %slice_reduce_fusion.own_ref), channel_id=1, source_target_pairs={{0,1},{1,0},{2,3},{3,2},{4,5},{5,4},{6,7},{7,6},{8,9},{9,8},{10,11... | collective-permute-start | bytes 98312 | tf_op jit(solution)/shard_map/ppermute | solution.py:484

commit v7 on v6

--- a/solution.py
+++ b/solution.py
@@ -313,25 +313,32 @@
     spectrum = jnp.concatenate([spectrum[8 * k : 8 * k + 4] for k in range(32)], axis=0)
     spectrum = spectrum.T
     far = jnp.abs(gap[:HALF])
-    far = jnp.concatenate([far, far], axis=0)
     for sign in range(2):
         table = turned_ref[sign, :HALF]
         fixed = fixed_ref[sign]
-        total = jnp.zeros((COEFS, LANES), F32)
+        even = jnp.zeros((HALF, LANES), F32)
+        odd = jnp.zeros((HALF, LANES), F32)
         for start in range(0, 2 * ORDER + 1, 7):
-            rows = []
+            rows, lows = [], []
             for d in range(start, start + 7):
-                rows += [table * spectrum[d : d + 1], table * spectrum[64 + d : 65 + d]]
-            high, low = halves(jnp.concatenate(rows, axis=0))
+                low = ((d - ORDER) ** 2 - 1) // 8 * 8 if d > ORDER else 0
+                lows.append(low)
+                rows += [table[low:] * spectrum[d : d + 1], table[low:] * spectrum[64 + d : 65 + d]]
+            high, small = halves(jnp.concatenate(rows, axis=0))
             product = jnp.dot(
-                jnp.concatenate([high, low], axis=1), fixed, preferred_element_type=F32
+                jnp.concatenate([high, small], axis=1), fixed, preferred_element_type=F32
             )
             product = product[:, :LANES] + product[:, LANES:]
-            for k in range(7):
-                part = product[k * COEFS : (k + 1) * COEFS]
-                total = jnp.where(far == start + k, part, total)
-        out_ref[sign, 0, :HALF] = total[:HALF]
-        out_ref[sign, 1, :HALF] = jnp.where(gap[:HALF] < 0, -total[HALF:], total[HALF:])
+            at = 0
+            for k, low in enumerate(lows):
+                here, size = far[low:] == start + k, HALF - low
+                new_even = jnp.where(here, product[at : at + size], even[low:])
+                new_odd = jnp.where(here, product[at + size : at + 2 * size], odd[low:])
+                at += 2 * size
+                even = jnp.concatenate([even[:low], new_even], axis=0) if low else new_even
+                odd = jnp.concatenate([odd[:low], new_odd], axis=0) if low else new_odd
+        out_ref[sign, 0, :HALF] = even
+        out_ref[sign, 1, :HALF] = jnp.where(gap[:HALF] < 0, -odd, odd)
         out_ref[sign, :, HALF:] = jnp.zeros((2, 8, LANES), F32)
 
 

time: 71.9 us -> 71.7 us (level)
  transfers between devices with their start and end apart: 3 -> 3, of which waited for: 2 -> 2; matrix products, arithmetic and copies ran while one was open for 2% -> 2% of each run, Pallas kernels for 7% -> 6%
where the time goes in v7:
time: 71.7 us; the launch traced here: 71.3 us
  blocking collectives  29.8 us (42%)
  Pallas kernels  16.1 us (22%)
  starting transfers between devices  12.6 us (18%)
  waiting for transfers between devices  8.59 us (12%)
  other arithmetic  2.33 us (3%)
  local copies, waits for them, and re-layouts  1.1 us (2%)
  between operations  0.72 us (1%)
    all_to_all x1, blocking collectives, shards(): line = lax.all_to_all(spread, LINE, 0, 0, tiled=True)  17.5 us
    all_to_all x1, blocking collectives, shards(): got = lax.all_to_all(messages, PLANE, 0, 0, tiled=True)  12.3 us
    pallas_call x1, Pallas kernels, moved_sum(): pl.pallas_call(functools.partial(move_kernel, unroll), in_specs=[smem, hb...  9.61 us
    all_to_all x1, waiting for transfers between devices, shards(): got = lax.all_to_all(packed, PLANE, 0, 0, tiled=True)  7.54 us
    pallas_call x6, Pallas kernels, call(): pl.pallas_call(body, out_shape=[jax.ShapeDtypeStruct(o.shape, o.dtype) fo...  6.53 us
    all_to_all x1, starting transfers between devices, shards(): got = lax.all_to_all(packed, PLANE, 0, 0, tiled=True)  5.03 us
    ppermute x1, starting transfers between devices, shards(): partner = lax.ppermute(own, PAIR, [(0, 1), (1, 0)])  4.25 us
    ppermute x1, starting transfers between devices, shards(): other = lax.ppermute(theirs, PAIR, [(0, 1), (1, 0)])  3.31 us
  transfers between devices with their start and end apart: 3, of which 2 were waited for; matrix products, arithmetic and copies ran while one was open for 2% of the time, Pallas kernels for 6%

profile of v7, /device:TPU:1, one launch (start us, length us, event | category | flops | bytes accessed | tf_op | source)
XLA Modules:
  0.0 71.3 jit_solution(11016639906147422990)
XLA Ops:
  0.6 0.7 convert_bitcast_fusion
  1.3 0.7 select_maximum_fusion.weight_ref
  2.0 0.0 copy-start
  2.0 0.0 copy-start.1
  2.0 9.6 %move.1 = (f32[2,256,512]{2,1,0:T(8,128)S(1)}, f32[16,64,128]{2,1,0:T(8,128)S(1)}) custom-call(s32[1]{0:T(128)} %bitcast.core_ref, bf16[8,240,1024]{2,1,0:T(8,128)(2,1)} %coef_hbm.1, bf16[3,8,480,240]{3,2,1,0:T(8,128)(2,1)} %table_hbm.1, f32[16,256]{1,0:T(8,128)S(1)} %select_maximum_fusion.weight_ref), custom_call_target="tpu_custom_call" | custom-call | flops 6000000000 | bytes 10000000 | tf_op jit(solution)/shard_map/move/pallas_call | solution.py:217
  11.6 3.3 %collective-permute-start = (f32[16,64,128]{2,1,0:T(8,128)S(1)}, f32[16,64,128]{2,1,0:T(8,128)S(1)}, u32[]{:S(2)}, u32[]{:S(2)}) collective-permute-start(f32[16,64,128]{2,1,0:T(8,128)S(1)} %get-tuple-element.32), channel_id=1, source_target_pairs={{0,1},{1,0},{2,3},{3,2},{4,5},{5,4},{6,7},{7,6},{8,9},{9,8},{10,11... | collective-permute-start | bytes 1572872 | tf_op jit(solution)/shard_map/ppermute | solution.py:455
  15.0 0.0 copy-done
  15.0 0.5 shard_map.86
  15.4 1.1 %collective-permute-done = f32[16,64,128]{2,1,0:T(8,128)S(1)} collective-permute-done((f32[16,64,128]{2,1,0:T(8,128)S(1)}, f32[16,64,128]{2,1,0:T(8,128)S(1)}, u32[]{:S(2)}, u32[]{:S(2)}) %collective-permute-start) | collective-permute-done | bytes 524320 | tf_op jit(solution)/shard_map/ppermute | solution.py:455
  16.5 0.9 %add.21 = f32[16,64,128]{2,1,0:T(8,128)} add(f32[16,64,128]{2,1,0:T(8,128)S(1)} %shard_map.86, f32[16,64,128]{2,1,0:T(8,128)S(1)} %collective-permute-done) | non-fusion elementwise | flops 131072 | bytes 1572864 | tf_op jit(solution)/shard_map/add | solution.py:463
  17.3 5.0 %all-to-all-start = ((f32[16,64,128]{2,1,0:T(8,128)}), f32[16,64,128]{2,1,0:T(8,128)S(1)}, u32[]{:S(2)}, u32[]{:S(2)}) async-start(f32[16,64,128]{2,1,0:T(8,128)} %add.21), calls=%async_computation | async-start | bytes 1048576 | tf_op jit(solution)/shard_map/all_to_all | solution.py:485
  22.4 0.1 pad_add_fusion.place_ref
  22.5 0.0 copy-done.1
  22.5 2.0 %shard_map.87 = (bf16[512,512]{1,0:T(8,128)(2,1)S(1)}, bf16[512,512]{1,0:T(8,128)(2,1)S(1)}, f32[2,128,128]{2,1,0:T(8,128)S(1)}, bf16[2,256,256]{2,1,0:T(8,128)(...) custom-call(s32[2]{0:T(128)S(1)} %pad_add_fusion.place_ref, ...), custom_call_target="tpu_custom_call" | custom-call | flops 100000000 | bytes 1785864 | tf_op jit(solution)/shard_map/pallas_call | solution.py:101
  24.5 1.1 %constant_dynamic-slice_fusion = (f32[240,32]{1,0:T(8,128)S(1)}, f32[240,32]{1,0:T(8,128)S(1)}) fusion(f32[240,1024]{1,0:T(8,128)} %param.11, s32[]{:T(128)S(6)} %select_n.7, s32[]{:T(128)S(6)} %select_n.6), kind=kLoop, calls=%fused_computation.6 | loop fusion | bytes 122888 | tf_op jit(solution)/shard_map/dynamic_slice | solution.py:482
  25.6 7.5 %all-to-all-done.got_ref = f32[16,64,128]{2,1,0:T(8,128)S(1)} async-done(((f32[16,64,128]{2,1,0:T(8,128)}), f32[16,64,128]{2,1,0:T(8,128)S(1)}, u32[]{:S(2)}, u32[]{:S(2)}) %all-to-all-start) | async-done | bytes 524320 | tf_op jit(solution)/shard_map/all_to_all | solution.py:485
  33.1 0.1 shard_map.88
  33.2 17.5 %all_to_all.15.line_ref = f32[8,72,128]{2,1,0:T(8,128)S(1)} all-to-all(f32[8,72,128]{2,1,0:T(8,128)S(1)} %shard_map.88), channel_id=1, replica_groups=mesh['sph_0'=4,'sph_1'=8,'ang_0'=4,'ang_1'=2] {'sph_1'}, dimensions={0} | all-to-all | bytes 589824 | tf_op jit(solution)/shard_map/all_to_all | solution.py:489
  50.7 4.2 %collective-permute-start.1 = (f32[64,128]{1,0:T(8,128)S(1)}, f32[64,128]{1,0:T(8,128)S(1)}, u32[]{:S(2)}, u32[]{:S(2)}) collective-permute-start(f32[64,128]{1,0:T(8,128)S(1)} %slice_reduce_fusion.own_ref), channel_id=1, source_target_pairs={{0,1},{1,0},{2,3},{3,2},{4,5},{5,4},{6,7},{7,6},{8,9},{9,8},{10,11... | collective-permute-start | bytes 98312 | tf_op jit(solution)/shard_map/ppermute | solution.py:491
  55.0 2.1 %shard_map.89.form_ref = f32[2,2,128,128]{3,2,1,0:T(8,128)S(1)} custom-call(f32[2,128,128]{2,1,0:T(8,128)S(1)} %get-tuple-element.51.turned_ref, bf16[2,256,256]{2,1,0:T(8,128)(2,1)S(1)} %get-tuple-element.52.fixed_ref, f32[8,72,128]{2,1,0:T(8,128)S(1)} %all_to_all.15.line_ref, f32[128,256]{1,0:T(8,128)S(1)} %get-tuple-element.53.waves_ref, ...), custom_call_target="tpu_custom_call" | custom-call | flops 1000000000 | bytes 1146880 | tf_op jit(solution)/shard_map/pallas_call | solution.py:101
  57.1 0.0 collective-permute-done.1.other_ref
  57.1 0.9 %shard_map.90 = f32[16,40,128]{2,1,0:T(8,128)S(1)} custom-call(s32[1]{0:T(128)} %bitcast.3.core_ref, f32[64,128]{1,0:T(8,128)S(1)} %slice_reduce_fusion.own_ref, f32[64,128]{1,0:T(8,128)S(1)} %collective-permute-done.1.other_ref, bf16[512,512]{1,0:T(8,128)(2,1)S(1)} %get-tuple-element.49.high_ref, bf16[512,512]{1,0:T(8,128)(2,1)S(1)} %get-tuple-element.50.low_ref, ...), custom_call_target="tpu_custom_call" | custom-call | flops 400000000 | bytes 1896452 | tf_op jit(solution)/shard_map/pallas_call | solution.py:101
  58.0 12.3 %all_to_all.16.got_ref = f32[16,40,128]{2,1,0:T(8,128)S(1)} all-to-all(f32[16,40,128]{2,1,0:T(8,128)S(1)} %shard_map.90), channel_id=1, replica_groups=mesh['sph_0'=4,'sph_1'=8,'ang_0'=4,'ang_1'=2] {'ang_0','sph_0'}, dimensions={0} | all-to-all | bytes 655360 | tf_op jit(solution)/shard_map/all_to_all | solution.py:505
  70.3 1.0 %shard_map.91 = (f32[4,32,512]{2,1,0:T(8,128)}, f32[3,64]{1,0:T(4,128)}) custom-call(s32[1]{0:T(128)} %bitcast.4.place_ref, f32[16,40,128]{2,1,0:T(8,128)S(1)} %all_to_all.16.got_ref), custom_call_target="tpu_custom_call" | custom-call | flops 1 | bytes 590596 | tf_op jit(solution)/shard_map/pallas_call | solution.py:101
  (1 shorter events, 0.0 us)
Async XLA Ops:
  2.0 12.9 %copy-start = (f32[4,64]{1,0:T(4,128)S(1)}, f32[4,64]{1,0:T(4,128)}, u32[]{:S(2)}) copy-start(f32[4,64]{1,0:T(4,128)} %detector_ref.1) | copy-start | bytes 3076
  2.0 20.5 %copy-start.1 = (f32[32,128]{1,0:T(8,128)S(1)}, f32[32,128]{1,0:T(8,128)}, u32[]{:S(2)}) copy-start(f32[32,128]{1,0:T(8,128)} %constant.35.clone.const_ref) | copy-start | bytes 49156
  11.6 4.8 %collective-permute-start = (f32[16,64,128]{2,1,0:T(8,128)S(1)}, f32[16,64,128]{2,1,0:T(8,128)S(1)}, u32[]{:S(2)}, u32[]{:S(2)}) collective-permute-start(f32[16,64,128]{2,1,0:T(8,128)S(1)} %get-tuple-element.32), channel_id=1, source_target_pairs={{0,1},{1,0},{2,3},{3,2},{4,5},{5,4},{6,7},{7,6},{8,9},{9,8},{10,11... | collective-permute-start | bytes 1572872 | tf_op jit(solution)/shard_map/ppermute | solution.py:455
  17.3 15.8 %all-to-all-start = ((f32[16,64,128]{2,1,0:T(8,128)}), f32[16,64,128]{2,1,0:T(8,128)S(1)}, u32[]{:S(2)}, u32[]{:S(2)}) async-start(f32[16,64,128]{2,1,0:T(8,128)} %add.21), calls=%async_computation | async-start | bytes 1048576 | tf_op jit(solution)/shard_map/all_to_all | solution.py:485
  50.7 6.4 %collective-permute-start.1 = (f32[64,128]{1,0:T(8,128)S(1)}, f32[64,128]{1,0:T(8,128)S(1)}, u32[]{:S(2)}, u32[]{:S(2)}) collective-permute-start(f32[64,128]{1,0:T(8,128)S(1)} %slice_reduce_fusion.own_ref), channel_id=1, source_target_pairs={{0,1},{1,0},{2,3},{3,2},{4,5},{5,4},{6,7},{7,6},{8,9},{9,8},{10,11... | collective-permute-start | bytes 98312 | tf_op jit(solution)/shard_map/ppermute | solution.py:491
